TPU v7x, 32 devices: a whole 2x2x4 slice. The times are simulated.
32 devices in a mesh: patch: 16 (over z, x, core), lev: 2 (over y).
Axes of the slice: x: 2, y: 2, z: 4, core: 2. Of those that a mesh axis runs over, the one named last changes fastest.
Arguments:
- fields: bfloat16 [8, 32, 32768], P(None, 'lev', 'patch'), may hold values from -6 to 6
- interp: bfloat16 [128, 128, 256], P('patch'), may hold values from -0.375 to 0.375
- conv_weight: bfloat16 [128, 8, 128, 128], P('patch'), may hold values from -0.1875 to 0.1875
- vert_weight: float32 [32, 5], replicated, may hold values from 0.1 to 0.5
- send_tiles: int32 [16, 4, 2], P('patch'), may hold values from 0 to 8, as said below
- tile_pattern: int32 [128, 8], P('patch'), may hold values from 0 to 15, as said below
Outputs:
- localized: float32 [8, 32, 32768], P(None, 'lev', 'patch')
Inputs may be any that keep to these rules, and one draw needn't show every extreme that they name: `send_tiles`: in every draw some link carries 2 tiles; every link carries at least one tile; the tiles of one link are distinct. `tile_pattern`: each row names distinct entries, each an own tile or a filled received slot.
All inputs are finite; a program needn't handle non-finite values.
Results may differ from a plain program's by a relative error of at most 0.0048.
Values may be sent and summed in bfloat16 or wider, within the bound.
A program may use at most 64 MiB of HBM per device.

v0:
```python
import functools

import jax
import jax.numpy as jnp
from jax import lax
from jax.experimental import pallas as pl
from jax.experimental.pallas import tpu as pltpu
from jax.sharding import PartitionSpec as P

MESH = pl.DeviceIdType.MESH
F32 = jnp.float32
BF16 = jnp.bfloat16


def link_offsets(reach_len):
    return [
        position - reach_len if position < reach_len else position - reach_len + 1
        for position in range(2 * reach_len)
    ]


def dot_t(left, right):
    return lax.dot_general(left, right, (((1,), (1,)), ((), ())), preferred_element_type=F32)


def kernel(
    n_patch,
    n_lev,
    fields_hbm,
    interp_hbm,
    conv_hbm,
    weight,
    send,
    pattern,
    out,
    fields,
    interp,
    conv,
    coarse,
    levels,
    middle,
    halo_out,
    halo_in,
    own,
    mixed,
    which,
    slot_of,
    load_sem,
    halo_sem,
    back_sem,
    forth_sem,
    *parts,
):
    members, level_len, _ = fields.shape
    tiles, tile_len, fine = interp.shape
    k_len = conv_hbm.shape[1]
    most, link_len = send.shape[1], send.shape[2]
    half = (weight.shape[0] - 1) // 2
    wide = 2 * half
    rows = members * level_len
    total_levels = weight.shape[1]
    offsets = link_offsets(link_len // 2)
    smooth, ext, links = parts[:2], parts[2:4], parts[4:]
    returning, arrived_back, sending, arrived = (
        [links[(2 * i + c) * link_len : (2 * i + c + 1) * link_len] for c in range(2)]
        for i in range(4)
    )
    edge = wide * members
    part_rows = (rows - 2 * edge, 2 * edge)
    me_p, me_l = lax.axis_index("patch"), lax.axis_index("lev")
    partner = [lax.rem(me_p + d + n_patch, n_patch) for d in offsets]
    source = [lax.rem(me_p - d + n_patch, n_patch) for d in offsets]
    order = sorted(range(link_len), key=lambda o: -abs(offsets[o]))

    load_f = pltpu.make_async_copy(fields_hbm, fields, load_sem.at[0])
    load_i = pltpu.make_async_copy(interp_hbm, interp, load_sem.at[1])
    load_c = pltpu.make_async_copy(conv_hbm, conv.at[:, pl.ds(0, k_len)], load_sem.at[2])
    load_f.start()
    load_i.start()

    barrier = pltpu.get_barrier_semaphore()
    for other in partner:
        pl.semaphore_signal(barrier, inc=1, device_id={"patch": other}, device_id_type=MESH)

    @pl.when(me_l > 0)
    def _():
        pl.semaphore_signal(barrier, inc=1, device_id={"lev": me_l - 1}, device_id_type=MESH)

    @pl.when(me_l < n_lev - 1)
    def _():
        pl.semaphore_signal(barrier, inc=1, device_id={"lev": me_l + 1}, device_id_type=MESH)

    @pl.loop(0, tiles)
    def _(t):
        named = [pattern[t, k] for k in range(k_len)]
        for e in range(tiles + link_len * most):
            index = jnp.int32(k_len)
            for k in range(k_len):
                index = jnp.where(named[k] == e, k, index)
            which[t, e] = index
        for o in range(link_len):
            index = jnp.int32(most)
            for s in range(most):
                index = jnp.where(send[0, s, o] == t, s, index)
            slot_of[t, o] = index
        conv[t, k_len] = jnp.zeros((tile_len, tile_len), BF16)

    load_c.start()
    for c in range(2):
        for o in range(link_len):
            arrived_back[c][o][most] = jnp.zeros((part_rows[c], tile_len), BF16)
        ext[c][tiles] = jnp.zeros((part_rows[c], tile_len), BF16)

    load_f.wait()
    load_i.wait()
    for t in range(tiles):
        block = fields[:, :, t * fine : (t + 1) * fine].reshape(rows, fine)
        coarse[t] = dot_t(block, interp[t])
        for l in range(level_len):
            levels[wide + l, t] = coarse[t, pl.ds(l, members, stride=level_len), :]
    for i in range(wide // 2):
        low = jnp.concatenate([levels[wide + 2 * i], levels[wide + 2 * i + 1]], axis=1)
        top = level_len + 2 * i
        high = jnp.concatenate([levels[top], levels[top + 1]], axis=1)
        halo_out[0, i] = low.astype(BF16)
        halo_out[1, i] = high.astype(BF16)

    down = pltpu.make_async_remote_copy(
        halo_out.at[0],
        halo_in.at[1],
        halo_sem.at[0],
        halo_sem.at[1],
        device_id={"lev": lax.rem(me_l + n_lev - 1, n_lev)},
        device_id_type=MESH,
    )
    up = pltpu.make_async_remote_copy(
        halo_out.at[1],
        halo_in.at[0],
        halo_sem.at[2],
        halo_sem.at[3],
        device_id={"lev": lax.rem(me_l + 1, n_lev)},
        device_id_type=MESH,
    )
    start = me_l * level_len

    def coefficient(level, column):
        return weight[column, jnp.clip(start + level, 0, total_levels - 1)]

    def adjoint_level(level):
        value = coefficient(level - half, wide) * levels[wide + level - half]
        for e in range(1 - half, half + 1):
            value = value + coefficient(level + e, half - e) * levels[wide + level + e]
        if level < 0:
            value = jnp.where(start + level >= 0, value, 0.0)
        if level >= level_len:
            value = jnp.where(start + level < total_levels, value, 0.0)
        middle[half + level] = value

    def forward_pair(level):
        both = []
        for l in (level, level + 1):
            value = coefficient(l, 0) * middle[l]
            for j in range(1, wide + 1):
                value = value + coefficient(l, j) * middle[l + j]
            both.append(value)
        pair = jnp.concatenate(both, axis=1).astype(BF16)
        if wide <= level < level_len - wide:
            smooth[0][:, pl.ds((level - wide) * members, 2 * members), :] = pair
        else:
            place = level if level < wide else level - level_len + 2 * wide
            smooth[1][:, pl.ds(place * members, 2 * members), :] = pair

    for level in range(half, level_len - half):
        adjoint_level(level)
    for level in range(wide, level_len - wide, 2):
        forward_pair(level)

    load_c.wait()

    def gathered(left, first):
        right = jnp.concatenate(
            [
                jnp.concatenate([conv[t, which[t, first + s]] for t in range(tiles)], axis=1)
                for s in range(most)
            ],
            axis=0,
        )
        return dot_t(left, right)

    def side_by_side(ref, count):
        return jnp.concatenate([ref[i] for i in range(count)], axis=1)

    def sum_back(c, o):
        sums = gathered(side_by_side(smooth[c], tiles), tiles + o * most).astype(BF16)
        for s in range(most):
            returning[c][o][s] = sums[:, s * tile_len : (s + 1) * tile_len]

    def send_back(c, o):
        copy = pltpu.make_async_remote_copy(
            returning[c][o],
            arrived_back[c][o].at[pl.ds(0, most)],
            back_sem.at[0, c, o],
            back_sem.at[1, c, o],
            device_id={"patch": source[o]},
            device_id_type=MESH,
        )
        copy.start()
        return copy

    def sum_own(c):
        low = 0 if c == 0 else part_rows[0]
        left = side_by_side(smooth[c], tiles)
        for first in range(0, tiles, most):
            sums = gathered(left, first)
            for s in range(most):
                own[first + s, pl.ds(low, part_rows[c])] = sums[
                    :, s * tile_len : (s + 1) * tile_len
                ]

    def send_forth(c):
        low = 0 if c == 0 else part_rows[0]
        for t in range(tiles):
            value = own[t, low : low + part_rows[c]]
            for o in range(link_len):
                value = value + arrived_back[c][o][slot_of[t, o]].astype(F32)
            ext[c][t] = value.astype(BF16)
        copies = {}
        for o in order:
            for s in range(most):
                sending[c][o][s] = ext[c][send[0, s, o]]
            copies[o] = pltpu.make_async_remote_copy(
                sending[c][o],
                arrived[c][o],
                forth_sem.at[0, c, o],
                forth_sem.at[1, c, o],
                device_id={"patch": partner[o]},
                device_id_type=MESH,
            )
            copies[o].start()
        return copies

    def spread(left, first, count, t):
        right = jnp.concatenate(
            [
                jnp.concatenate([conv[u, which[u, first + e]] for e in range(count)], axis=0)
                for u in (t, t + 1)
            ],
            axis=1,
        )
        return jnp.dot(left, right, preferred_element_type=F32)

    def places(c):
        if c == 0:
            return [(0, part_rows[0], edge)]
        return [(0, edge, 0), (edge, edge, rows - edge)]

    def put(c, t, sums, fresh):
        for begin, count, place in places(c):
            for i in range(2):
                value = sums[begin : begin + count, i * tile_len : (i + 1) * tile_len]
                if not fresh:
                    value = value + mixed[t + i, pl.ds(place, count)]
                mixed[t + i, pl.ds(place, count)] = value

    def mix_own(c):
        left = side_by_side(ext[c], tiles)
        for t in range(0, tiles, 2):
            put(c, t, spread(left, 0, tiles, t), True)

    def mix_link(c, o):
        left = side_by_side(arrived[c][o], most)
        for t in range(0, tiles, 2):
            put(c, t, spread(left, tiles + o * most, most, t), False)

    for o in order:
        sum_back(0, o)
    beside = jnp.where(me_l > 0, 1, 0) + jnp.where(me_l < n_lev - 1, 1, 0)
    pl.semaphore_wait(barrier, link_len + beside)

    @pl.when(me_l > 0)
    def _():
        down.start()

    @pl.when(me_l < n_lev - 1)
    def _():
        up.start()

    back = [{o: send_back(0, o) for o in order}, {}]
    sum_own(0)

    def unpack(side, base):
        for i in range(wide // 2):
            pair = halo_in[side, i].astype(F32)
            levels[base + 2 * i] = pair[:, :members]
            levels[base + 2 * i + 1] = pair[:, members:]

    def clear(base):
        for i in range(wide):
            levels[base + i] = jnp.zeros(levels.shape[1:], F32)

    @pl.when(me_l > 0)
    def _():
        up.wait_recv()
        unpack(0, 0)

    @pl.when(me_l == 0)
    def _():
        clear(0)

    @pl.when(me_l < n_lev - 1)
    def _():
        down.wait_recv()
        unpack(1, wide + level_len)

    @pl.when(me_l == n_lev - 1)
    def _():
        clear(wide + level_len)

    for level in list(range(-half, half)) + list(range(level_len - half, level_len + half)):
        adjoint_level(level)
    for level in list(range(0, wide, 2)) + list(range(level_len - wide, level_len, 2)):
        forward_pair(level)

    for o in order:
        sum_back(1, o)
        back[1][o] = send_back(1, o)
    sum_own(1)
    forth = []
    for c in range(2):
        for o in order:
            back[c][o].wait_recv()
        forth.append(send_forth(c))
        mix_own(c)
    for c in range(2):
        for o in order[::-1]:
            forth[c][o].wait_recv()
            mix_link(c, o)
    for t in range(tiles):
        part = jnp.concatenate(
            [mixed[t, pl.ds(m, level_len, stride=members), :] for m in range(members)], axis=0
        ).astype(BF16)
        result = jnp.dot(part, interp[t], preferred_element_type=F32)
        out[:, :, t * fine : (t + 1) * fine] = result.reshape(members, level_len, fine)
    for copies in back + forth:
        for o in order:
            copies[o].wait_send()

    @pl.when(me_l > 0)
    def _():
        down.wait_send()

    @pl.when(me_l < n_lev - 1)
    def _():
        up.wait_send()


def solution(mesh):
    n_patch, n_lev = mesh.shape["patch"], mesh.shape["lev"]

    def shards(fields, interp, conv_weight, vert_weight, send_tiles, tile_pattern):
        members, level_len, column_len = fields.shape
        tiles, tile_len, fine = interp.shape
        k_len = conv_weight.shape[1]
        link_len, most = send_tiles.shape[1:]
        wide = vert_weight.shape[1] - 1
        rows = members * level_len
        any_spec = pl.BlockSpec(memory_space=pl.ANY)
        smem_spec = pl.BlockSpec(memory_space=pltpu.SMEM)

        edge = 2 * wide * members

        def per_part(count, copies):
            return [
                pltpu.VMEM((count, part_rows, tile_len), BF16)
                for part_rows in (rows - edge, edge)
                for _ in range(copies)
            ]

        return pl.pallas_call(
            functools.partial(kernel, n_patch, n_lev),
            name="localize",
            out_shape=pltpu.VMEM(fields.shape, F32),
            in_specs=[any_spec] * 3 + [smem_spec] * 3,
            out_specs=pl.BlockSpec(memory_space=pltpu.VMEM),
            scratch_shapes=[
                pltpu.VMEM(fields.shape, BF16),
                pltpu.VMEM(interp.shape, BF16),
                pltpu.VMEM((tiles, k_len + 1, tile_len, tile_len), BF16),
                pltpu.VMEM((tiles, rows, tile_len), F32),
                pltpu.VMEM((level_len + 2 * wide, tiles, members, tile_len), F32),
                pltpu.VMEM((level_len + wide, tiles, members, tile_len), F32),
                pltpu.VMEM((2, wide // 2, tiles, 2 * members, tile_len), BF16),
                pltpu.VMEM((2, wide // 2, tiles, 2 * members, tile_len), BF16),
                pltpu.VMEM((tiles, rows, tile_len), F32),
                pltpu.VMEM((tiles, rows, tile_len), F32),
                pltpu.SMEM((tiles, tiles + link_len * most), jnp.int32),
                pltpu.SMEM((tiles, link_len), jnp.int32),
                pltpu.SemaphoreType.DMA((3,)),
                pltpu.SemaphoreType.DMA((4,)),
                pltpu.SemaphoreType.DMA((2, 2, link_len)),
                pltpu.SemaphoreType.DMA((2, 2, link_len)),
            ]
            + per_part(tiles, 1)
            + per_part(tiles + 1, 1)
            + per_part(most, link_len)
            + per_part(most + 1, link_len)
            + per_part(most, link_len)
            + per_part(most, link_len),
            compiler_params=pltpu.CompilerParams(collective_id=0, has_side_effects=True),
        )(fields, interp, conv_weight, vert_weight.T, send_tiles.transpose(0, 2, 1), tile_pattern)

    in_specs = (
        P(None, "lev", "patch"),
        P("patch", None, None),
        P("patch", None, None, None),
        P(),
        P("patch", None, None),
        P("patch", None),
    )
    out_specs = P(None, "lev", "patch")
    return jax.shard_map(shards, mesh=mesh, in_specs=in_specs, out_specs=out_specs, check_vma=False)
```

profile of v0, /device:TPU:0, one launch (start us, length us, event | category | flops | bytes accessed | tf_op | source)
XLA Modules:
  0.0 22.8 jit_solution(4238844695878587356)
XLA Ops:
  0.0 21.8 %localize.1 = f32[8,16,2048]{2,1,0:T(8,128)S(1)} custom-call(bf16[8,16,2048]{2,1,0:T(8,128)(2,1)} %fields_hbm.1, bf16[8,128,256]{2,1,0:T(8,128)(2,1)} %interp_hbm.1, bf16[8,8,128,128]{3,2,1,0:T(8,128)(2,1)} %conv_hbm.1, f32[5,32]{1,0:T(8,128)} %bitcast.2, s32[1,2,4]{2,1,0:T(2,128)} %bitcast.3, s32[8,8]{1,0:T(8,128)} %pattern.1), custom_call_target="tpu_custom_call" | custom-call | tf_op jit(solution)/shard_map/localize/pallas_call | solution.py:379
  21.8 1.0 %copy.8 = f32[8,16,2048]{2,1,0:T(8,128)} copy(f32[8,16,2048]{2,1,0:T(8,128)S(1)} %localize.1) | data formatting | bytes 2097152
where the time goes:
time: 23 us; the launch traced here: 22.8 us
  Pallas kernels  21.8 us (95%)
  local copies, waits for them, and re-layouts  0.97 us (4%)
    pallas_call x1, Pallas kernels, shards(): pl.pallas_call(functools.partial(kernel, n_patch, n_lev), name='localize'...  21.8 us
    unnamed x1, local copies, waits for them, and re-layouts  0.97 us

commit v1 on v0

v1 whole, which is shorter than its diff:
```python
import functools

import jax
import jax.numpy as jnp
from jax import lax
from jax.experimental import pallas as pl
from jax.experimental.pallas import tpu as pltpu
from jax.sharding import PartitionSpec as P

MESH = pl.DeviceIdType.MESH
F32 = jnp.float32
BF16 = jnp.bfloat16


def link_offsets(reach_len):
    return [
        position - reach_len if position < reach_len else position - reach_len + 1
        for position in range(2 * reach_len)
    ]


def chunks_of(parts):
    chunks = []
    for low, count in parts:
        step = count // 2 if count % 32 == 0 else count
        chunks.append([(low + at, step) for at in range(0, count, step)])
    return chunks


def dot_t(left, right):
    return lax.dot_general(left, right, (((1,), (1,)), ((), ())), preferred_element_type=F32)


def kernel(
    n_patch,
    n_lev,
    fields_hbm,
    interp_hbm,
    conv_hbm,
    weight_hbm,
    send_hbm,
    pattern_hbm,
    out,
    weight,
    send,
    pattern,
    fields,
    interp,
    conv,
    coarse,
    levels,
    middle,
    halo_out,
    halo_in,
    own,
    mixed,
    smooth,
    ext,
    power,
    which,
    slot_of,
    load_sem,
    halo_sem,
    back_sem,
    forth_sem,
    enter_sem,
    enter_lev,
    *links,
):
    members, level_len, _ = fields.shape
    tiles, tile_len, fine = interp.shape
    k_len = conv_hbm.shape[1]
    most, link_len = send.shape[1], send.shape[2]
    half = (weight.shape[0] - 1) // 2
    wide = 2 * half
    rows = members * level_len
    total_levels = weight.shape[1]
    offsets = link_offsets(link_len // 2)
    returning, sending, arrived = (links[i * link_len : (i + 1) * link_len] for i in range(3))
    arrived_back = [links[i * link_len : (i + 1) * link_len] for i in range(3, len(links) // link_len)]
    edge = wide * members
    parts = [(0, rows - 2 * edge), (rows - 2 * edge, 2 * edge)]
    chunks = chunks_of(parts)
    numbered = [(low, count) for part in chunks for low, count in part]
    me_p, me_l = lax.axis_index("patch"), lax.axis_index("lev")
    partner = [lax.rem(me_p + d + n_patch, n_patch) for d in offsets]
    source = [lax.rem(me_p - d + n_patch, n_patch) for d in offsets]
    opposite = [offsets.index(-d) for d in offsets]
    upper = sorted((o for o in range(link_len) if offsets[o] < 0), key=lambda o: offsets[o])
    lower = sorted((o for o in range(link_len) if offsets[o] > 0), key=lambda o: -offsets[o])

    load_w = pltpu.make_async_copy(weight_hbm, weight, load_sem.at[3])
    load_s = pltpu.make_async_copy(send_hbm, send, load_sem.at[4])
    load_p = pltpu.make_async_copy(pattern_hbm, pattern, load_sem.at[5])
    load_f = pltpu.make_async_copy(fields_hbm, fields, load_sem.at[0])
    load_i = pltpu.make_async_copy(interp_hbm, interp, load_sem.at[1])
    load_c = pltpu.make_async_copy(conv_hbm, conv.at[:, pl.ds(0, k_len)], load_sem.at[2])
    load_p.start()
    load_s.start()
    load_w.start()
    load_f.start()
    load_i.start()
    load_c.start()

    barrier = pltpu.get_barrier_semaphore()
    for o in range(link_len):

        @pl.when(partner[o] > me_p)
        def _(o=o):
            pl.semaphore_signal(
                barrier, inc=1, device_id={"patch": partner[o]}, device_id_type=MESH
            )

    @pl.when(me_l < n_lev - 1)
    def _():
        pl.semaphore_signal(barrier, inc=1, device_id={"lev": me_l + 1}, device_id_type=MESH)

    bits = k_len.bit_length()
    per_word = 31 // bits
    entries = tiles + link_len * most
    words = -(-entries // per_word)
    for e in range(entries):
        for w in range(words):
            inside = w * per_word <= e < (w + 1) * per_word
            power[w, e] = jnp.int32(1 << (bits * (e - w * per_word)) if inside else 0)
    for t in range(tiles):
        conv[t, k_len] = jnp.zeros((tile_len, tile_len), BF16)
    for i, (_, count) in enumerate(numbered):
        for o in range(link_len):
            arrived_back[i][o][most] = jnp.zeros((count, tile_len), BF16)
    ext[tiles] = jnp.zeros((rows, tile_len), BF16)
    load_p.wait()
    load_s.wait()
    load_w.wait()
    empty = sum(k_len << (bits * i) for i in range(per_word))
    for t in range(tiles):
        packed = [jnp.int32(empty) for _ in range(words)]
        for k in range(k_len):
            named = pattern[t, k]
            for w in range(words):
                packed[w] = packed[w] + jnp.int32(k - k_len) * power[w, named]
        for e in range(entries):
            w, place = e // per_word, bits * (e % per_word)
            which[t, e] = (packed[w] >> place) & ((1 << bits) - 1)
        for o in range(link_len):
            index = jnp.int32(most)
            for s in range(most):
                index = jnp.where(send[0, s, o] == t, s, index)
            slot_of[t, o] = index

    load_f.wait()
    load_i.wait()
    for t in range(tiles):
        block = fields[:, :, t * fine : (t + 1) * fine].reshape(rows, fine)
        coarse[t] = dot_t(block, interp[t])
        for l in range(level_len):
            levels[wide + l, t] = coarse[t, pl.ds(l, members, stride=level_len), :]
    for i in range(wide // 2):
        low = jnp.concatenate([levels[wide + 2 * i], levels[wide + 2 * i + 1]], axis=1)
        top = level_len + 2 * i
        high = jnp.concatenate([levels[top], levels[top + 1]], axis=1)
        halo_out[0, i] = low.astype(BF16)
        halo_out[1, i] = high.astype(BF16)

    down = pltpu.make_async_remote_copy(
        halo_out.at[0],
        halo_in.at[1],
        halo_sem.at[0],
        halo_sem.at[1],
        device_id={"lev": lax.rem(me_l + n_lev - 1, n_lev)},
        device_id_type=MESH,
    )
    up = pltpu.make_async_remote_copy(
        halo_out.at[1],
        halo_in.at[0],
        halo_sem.at[2],
        halo_sem.at[3],
        device_id={"lev": lax.rem(me_l + 1, n_lev)},
        device_id_type=MESH,
    )

    before = jnp.where(me_l > 0, 1, 0)
    for o in range(link_len):
        before = before + jnp.where(partner[o] < me_p, 1, 0)

    @pl.when(before > 0)
    def _():
        pl.semaphore_wait(barrier, before)

    for o in range(link_len):

        @pl.when(partner[o] < me_p)
        def _(o=o):
            pl.semaphore_signal(
                enter_sem.at[opposite[o]],
                inc=1,
                device_id={"patch": partner[o]},
                device_id_type=MESH,
            )

    @pl.when(me_l > 0)
    def _():
        pl.semaphore_signal(enter_lev, inc=1, device_id={"lev": me_l - 1}, device_id_type=MESH)
        down.start()

    @pl.when(me_l < n_lev - 1)
    def _():
        pl.semaphore_wait(enter_lev, 1)
        up.start()

    start = me_l * level_len

    def coefficient(level, column):
        return weight[column, jnp.clip(start + level, 0, total_levels - 1)]

    def adjoint_level(level):
        value = coefficient(level - half, wide) * levels[wide + level - half]
        for e in range(1 - half, half + 1):
            value = value + coefficient(level + e, half - e) * levels[wide + level + e]
        if level < 0:
            value = jnp.where(start + level >= 0, value, 0.0)
        if level >= level_len:
            value = jnp.where(start + level < total_levels, value, 0.0)
        middle[half + level] = value

    def forward_pair(level):
        both = []
        for l in (level, level + 1):
            value = coefficient(l, 0) * middle[l]
            for j in range(1, wide + 1):
                value = value + coefficient(l, j) * middle[l + j]
            both.append(value)
        pair = jnp.concatenate(both, axis=1).astype(BF16)
        if wide <= level < level_len - wide:
            place = (level - wide) * members
        else:
            place = level if level < wide else level - level_len + 2 * wide
            place = parts[1][0] + place * members
        smooth[:, pl.ds(place, 2 * members), :] = pair

    for level in range(half, level_len - half):
        adjoint_level(level)
    for level in range(wide, level_len - wide, 2):
        forward_pair(level)

    load_c.wait()

    def gathered(left, first):
        right = jnp.concatenate(
            [
                jnp.concatenate([conv[t, which[t, first + s]] for t in range(tiles)], axis=1)
                for s in range(most)
            ],
            axis=0,
        )
        return dot_t(left, right)

    def side_by_side(ref, count, low, size):
        return jnp.concatenate([ref[i, pl.ds(low, size)] for i in range(count)], axis=1)

    def sum_back(c, o):
        low, count = parts[c]
        left = side_by_side(smooth, tiles, low, count)
        sums = gathered(left, tiles + o * most).astype(BF16)
        for s in range(most):
            returning[o][s, pl.ds(low, count)] = sums[:, s * tile_len : (s + 1) * tile_len]

    def copy_back(o, i):
        low, count = numbered[i]
        return pltpu.make_async_remote_copy(
            returning[o].at[:, pl.ds(low, count)],
            arrived_back[i][o].at[pl.ds(0, most)],
            back_sem.at[0, i, o],
            back_sem.at[1, i, o],
            device_id={"patch": source[o]},
            device_id_type=MESH,
        )

    def copy_forth(o, i):
        low, count = numbered[i]
        return pltpu.make_async_remote_copy(
            sending[o].at[:, pl.ds(low, count)],
            arrived[o].at[:, pl.ds(low, count)],
            forth_sem.at[0, i, o],
            forth_sem.at[1, i, o],
            device_id={"patch": partner[o]},
            device_id_type=MESH,
        )

    def indices(c):
        first = len(chunks[0]) if c else 0
        return range(first, first + len(chunks[c]))

    def sum_own(c):
        low, count = parts[c]
        left = side_by_side(smooth, tiles, low, count)
        for first in range(0, tiles, most):
            sums = gathered(left, first)
            for s in range(most):
                own[first + s, pl.ds(low, count)] = sums[:, s * tile_len : (s + 1) * tile_len]

    def send_back(c):
        for o in upper:
            sum_back(c, o)
        if c == 0:
            for o in upper:

                @pl.when(source[o] > me_p)
                def _(o=o):
                    pl.semaphore_wait(enter_sem.at[opposite[o]], 1)

        for i in indices(c):
            for o in upper:
                copy_back(o, i).start()
        for o in lower:
            sum_back(c, o)
        for o in lower:

            @pl.when(source[o] < me_p)
            def _(o=o):
                for i in indices(c):
                    copy_back(o, i).start()

    send_back(0)
    sum_own(0)

    def unpack(side, base):
        for i in range(wide // 2):
            pair = halo_in[side, i].astype(F32)
            levels[base + 2 * i] = pair[:, :members]
            levels[base + 2 * i + 1] = pair[:, members:]

    def clear(base):
        for i in range(wide):
            levels[base + i] = jnp.zeros(levels.shape[1:], F32)

    @pl.when(me_l > 0)
    def _():
        up.wait_recv()
        unpack(0, 0)

    @pl.when(me_l == 0)
    def _():
        clear(0)

    @pl.when(me_l < n_lev - 1)
    def _():
        down.wait_recv()
        unpack(1, wide + level_len)

    @pl.when(me_l == n_lev - 1)
    def _():
        clear(wide + level_len)

    for level in list(range(-half, half)) + list(range(level_len - half, level_len + half)):
        adjoint_level(level)
    for level in list(range(0, wide, 2)) + list(range(level_len - wide, level_len, 2)):
        forward_pair(level)

    send_back(1)
    for o in lower:

        @pl.when(source[o] > me_p)
        def _(o=o):
            pl.semaphore_wait(enter_sem.at[opposite[o]], 1)
            for i in range(len(numbered)):
                copy_back(o, i).start()

    sum_own(1)

    for i, (low, count) in enumerate(numbered):
        for o in upper + lower:
            copy_back(o, i).wait_recv()
        for t in range(tiles):
            value = own[t, pl.ds(low, count)]
            for o in range(link_len):
                value = value + arrived_back[i][o][slot_of[t, o]].astype(F32)
            ext[t, pl.ds(low, count)] = value.astype(BF16)
        for o in lower + upper:
            for s in range(most):
                sending[o][s, pl.ds(low, count)] = ext[send[0, s, o], pl.ds(low, count)]
            copy_forth(o, i).start()

    def spread(left, named, t):
        right = jnp.concatenate(
            [
                jnp.concatenate([conv[u, which[u, e]] for e in named], axis=0)
                for u in (t, t + 1)
            ],
            axis=1,
        )
        return jnp.dot(left, right, preferred_element_type=F32)

    def places():
        return [(0, parts[0][1], edge), (parts[1][0], edge, 0), (parts[1][0] + edge, edge, rows - edge)]

    def put(t, sums, fresh):
        for begin, count, place in places():
            for i in range(2):
                value = sums[begin : begin + count, i * tile_len : (i + 1) * tile_len]
                if not fresh:
                    value = value + mixed[t + i, pl.ds(place, count)]
                mixed[t + i, pl.ds(place, count)] = value

    left = side_by_side(ext, tiles, 0, rows)
    for t in range(0, tiles, 2):
        put(t, spread(left, range(tiles), t), True)
    for group in (upper, lower):
        for i in range(len(numbered)):
            for o in group:
                copy_forth(o, i).wait_recv()
        left = jnp.concatenate([side_by_side(arrived[o], most, 0, rows) for o in group], axis=1)
        named = [tiles + o * most + s for o in group for s in range(most)]
        for t in range(0, tiles, 2):
            put(t, spread(left, named, t), False)

    for t in range(tiles):
        part = jnp.concatenate(
            [mixed[t, pl.ds(m, level_len, stride=members), :] for m in range(members)], axis=0
        ).astype(BF16)
        result = jnp.dot(part, interp[t], preferred_element_type=F32)
        out[:, :, t * fine : (t + 1) * fine] = result.reshape(members, level_len, fine)
    for i in range(len(numbered)):
        for o in range(link_len):
            copy_back(o, i).wait_send()
            copy_forth(o, i).wait_send()

    @pl.when(me_l > 0)
    def _():
        down.wait_send()

    @pl.when(me_l < n_lev - 1)
    def _():
        up.wait_send()


def solution(mesh):
    n_patch, n_lev = mesh.shape["patch"], mesh.shape["lev"]

    def shards(fields, interp, conv_weight, vert_weight, send_tiles, tile_pattern):
        members, level_len, column_len = fields.shape
        tiles, tile_len, fine = interp.shape
        k_len = conv_weight.shape[1]
        link_len, most = send_tiles.shape[1:]
        wide = vert_weight.shape[1] - 1
        rows = members * level_len
        any_spec = pl.BlockSpec(memory_space=pl.ANY)
        entries = tiles + link_len * most
        words = -(-entries // (31 // k_len.bit_length()))
        weight, send = vert_weight.T, send_tiles.transpose(0, 2, 1)
        edge = 2 * wide * members
        sizes = [count for part in chunks_of([(0, rows - edge), (rows - edge, edge)]) for _, count in part]

        def per_link(count, size=rows):
            return [pltpu.VMEM((count, size, tile_len), BF16) for _ in range(link_len)]

        return pl.pallas_call(
            functools.partial(kernel, n_patch, n_lev),
            name="localize",
            out_shape=pltpu.VMEM(fields.shape, F32),
            in_specs=[any_spec] * 6,
            out_specs=pl.BlockSpec(memory_space=pltpu.VMEM),
            scratch_shapes=[
                pltpu.SMEM(weight.shape, F32),
                pltpu.SMEM(send.shape, jnp.int32),
                pltpu.SMEM(tile_pattern.shape, jnp.int32),
                pltpu.VMEM(fields.shape, BF16),
                pltpu.VMEM(interp.shape, BF16),
                pltpu.VMEM((tiles, k_len + 1, tile_len, tile_len), BF16),
                pltpu.VMEM((tiles, rows, tile_len), F32),
                pltpu.VMEM((level_len + 2 * wide, tiles, members, tile_len), F32),
                pltpu.VMEM((level_len + wide, tiles, members, tile_len), F32),
                pltpu.VMEM((2, wide // 2, tiles, 2 * members, tile_len), BF16),
                pltpu.VMEM((2, wide // 2, tiles, 2 * members, tile_len), BF16),
                pltpu.VMEM((tiles, rows, tile_len), F32),
                pltpu.VMEM((tiles, rows, tile_len), F32),
                pltpu.VMEM((tiles, rows, tile_len), BF16),
                pltpu.VMEM((tiles + 1, rows, tile_len), BF16),
                pltpu.SMEM((words, entries), jnp.int32),
                pltpu.SMEM((tiles, entries), jnp.int32),
                pltpu.SMEM((tiles, link_len), jnp.int32),
                pltpu.SemaphoreType.DMA((6,)),
                pltpu.SemaphoreType.DMA((4,)),
                pltpu.SemaphoreType.DMA((2, len(sizes), link_len)),
                pltpu.SemaphoreType.DMA((2, len(sizes), link_len)),
                pltpu.SemaphoreType.REGULAR((link_len,)),
                pltpu.SemaphoreType.REGULAR,
            ]
            + per_link(most)
            + per_link(most)
            + per_link(most)
            + [ref for size in sizes for ref in per_link(most + 1, size)],
            compiler_params=pltpu.CompilerParams(collective_id=0, has_side_effects=True),
        )(fields, interp, conv_weight, weight, send, tile_pattern)

    in_specs = (
        P(None, "lev", "patch"),
        P("patch", None, None),
        P("patch", None, None, None),
        P(),
        P("patch", None, None),
        P("patch", None),
    )
    out_specs = P(None, "lev", "patch")
    return jax.shard_map(shards, mesh=mesh, in_specs=in_specs, out_specs=out_specs, check_vma=False)
```

time: 23 us -> 20.4 us (0.89)
  Pallas kernels: 21.8 us -> 19.2 us
    pallas_call x1, Pallas kernels: 21.8 us -> 19.2 us  [shards(): pl.pallas_call(functools.partial(kernel, n_patch, n_lev), name='localize'...]
where the time goes in v1:
time: 20.4 us; the launch traced here: 20.2 us
  Pallas kernels  19.2 us (94%)
  local copies, waits for them, and re-layouts  0.97 us (5%)
    pallas_call x1, Pallas kernels, shards(): pl.pallas_call(functools.partial(kernel, n_patch, n_lev), name='localize'...  19.2 us
    unnamed x1, local copies, waits for them, and re-layouts  0.97 us

profile of v1, /device:TPU:0, one launch (start us, length us, event | category | flops | bytes accessed | tf_op | source)
XLA Modules:
  0.0 20.2 jit_solution(165500555830490156)
XLA Ops:
  0.0 19.2 %localize.1 = f32[8,16,2048]{2,1,0:T(8,128)S(1)} custom-call(bf16[8,16,2048]{2,1,0:T(8,128)(2,1)} %fields_hbm.1, bf16[8,128,256]{2,1,0:T(8,128)(2,1)} %interp_hbm.1, bf16[8,8,128,128]{3,2,1,0:T(8,128)(2,1)} %conv_hbm.1, f32[5,32]{1,0:T(8,128)} %bitcast.2, s32[1,2,4]{2,1,0:T(2,128)} %bitcast.3, s32[8,8]{1,0:T(8,128)} %pattern_hbm.1), custom_call_target="tpu_custom_call" | custom-call | tf_op jit(solution)/shard_map/localize/pallas_call | solution.py:457
  19.2 1.0 %copy.8 = f32[8,16,2048]{2,1,0:T(8,128)} copy(f32[8,16,2048]{2,1,0:T(8,128)S(1)} %localize.1) | data formatting | bytes 2097152

commit v2 on v1

--- a/solution.py
+++ b/solution.py
@@ -61,11 +61,15 @@
     slot_of,
     load_sem,
     halo_sem,
+    send_sem,
     back_sem,
     forth_sem,
     enter_sem,
     enter_lev,
-    *links,
+    returning,
+    sending,
+    arrived,
+    *arrived_back,
 ):
     members, level_len, _ = fields.shape
     tiles, tile_len, fine = interp.shape
@@ -76,8 +80,6 @@
     rows = members * level_len
     total_levels = weight.shape[1]
     offsets = link_offsets(link_len // 2)
-    returning, sending, arrived = (links[i * link_len : (i + 1) * link_len] for i in range(3))
-    arrived_back = [links[i * link_len : (i + 1) * link_len] for i in range(3, len(links) // link_len)]
     edge = wide * members
     parts = [(0, rows - 2 * edge), (rows - 2 * edge, 2 * edge)]
     chunks = chunks_of(parts)
@@ -85,7 +87,6 @@
     me_p, me_l = lax.axis_index("patch"), lax.axis_index("lev")
     partner = [lax.rem(me_p + d + n_patch, n_patch) for d in offsets]
     source = [lax.rem(me_p - d + n_patch, n_patch) for d in offsets]
-    opposite = [offsets.index(-d) for d in offsets]
     upper = sorted((o for o in range(link_len) if offsets[o] < 0), key=lambda o: offsets[o])
     lower = sorted((o for o in range(link_len) if offsets[o] > 0), key=lambda o: -offsets[o])
 
@@ -127,11 +128,36 @@
         conv[t, k_len] = jnp.zeros((tile_len, tile_len), BF16)
     for i, (_, count) in enumerate(numbered):
         for o in range(link_len):
-            arrived_back[i][o][most] = jnp.zeros((count, tile_len), BF16)
+            arrived_back[i][o, most] = jnp.zeros((count, tile_len), BF16)
     ext[tiles] = jnp.zeros((rows, tile_len), BF16)
+    before = jnp.where(me_l > 0, 1, 0)
+    for o in range(link_len):
+        before = before + jnp.where(partner[o] < me_p, 1, 0)
+
+    @pl.when(before > 0)
+    def _():
+        pl.semaphore_wait(barrier, before)
+
+    for o in range(link_len):
+
+        @pl.when(partner[o] < me_p)
+        def _(o=o):
+            pl.semaphore_signal(
+                enter_sem.at[0 if offsets[o] < 0 else 1],
+                inc=1,
+                device_id={"patch": partner[o]},
+                device_id_type=MESH,
+            )
+
+    @pl.when(me_l > 0)
+    def _():
+        pl.semaphore_signal(enter_lev, inc=1, device_id={"lev": me_l - 1}, device_id_type=MESH)
+
     load_p.wait()
     load_s.wait()
     load_w.wait()
+    load_f.wait()
+    load_i.wait()
     empty = sum(k_len << (bits * i) for i in range(per_word))
     for t in range(tiles):
         packed = [jnp.int32(empty) for _ in range(words)]
@@ -147,9 +173,6 @@
             for s in range(most):
                 index = jnp.where(send[0, s, o] == t, s, index)
             slot_of[t, o] = index
-
-    load_f.wait()
-    load_i.wait()
     for t in range(tiles):
         block = fields[:, :, t * fine : (t + 1) * fine].reshape(rows, fine)
         coarse[t] = dot_t(block, interp[t])
@@ -179,28 +202,8 @@
         device_id_type=MESH,
     )
 
-    before = jnp.where(me_l > 0, 1, 0)
-    for o in range(link_len):
-        before = before + jnp.where(partner[o] < me_p, 1, 0)
-
-    @pl.when(before > 0)
-    def _():
-        pl.semaphore_wait(barrier, before)
-
-    for o in range(link_len):
-
-        @pl.when(partner[o] < me_p)
-        def _(o=o):
-            pl.semaphore_signal(
-                enter_sem.at[opposite[o]],
-                inc=1,
-                device_id={"patch": partner[o]},
-                device_id_type=MESH,
-            )
-
     @pl.when(me_l > 0)
     def _():
-        pl.semaphore_signal(enter_lev, inc=1, device_id={"lev": me_l - 1}, device_id_type=MESH)
         down.start()
 
     @pl.when(me_l < n_lev - 1)
@@ -263,15 +266,15 @@
         left = side_by_side(smooth, tiles, low, count)
         sums = gathered(left, tiles + o * most).astype(BF16)
         for s in range(most):
-            returning[o][s, pl.ds(low, count)] = sums[:, s * tile_len : (s + 1) * tile_len]
+            returning[o, s, pl.ds(low, count)] = sums[:, s * tile_len : (s + 1) * tile_len]
 
     def copy_back(o, i):
         low, count = numbered[i]
         return pltpu.make_async_remote_copy(
-            returning[o].at[:, pl.ds(low, count)],
-            arrived_back[i][o].at[pl.ds(0, most)],
-            back_sem.at[0, i, o],
-            back_sem.at[1, i, o],
+            returning.at[o, :, pl.ds(low, count)],
+            arrived_back[i].at[o, pl.ds(0, most)],
+            send_sem.at[0],
+            back_sem.at[i],
             device_id={"patch": source[o]},
             device_id_type=MESH,
         )
@@ -279,11 +282,32 @@
     def copy_forth(o, i):
         low, count = numbered[i]
         return pltpu.make_async_remote_copy(
-            sending[o].at[:, pl.ds(low, count)],
-            arrived[o].at[:, pl.ds(low, count)],
-            forth_sem.at[0, i, o],
-            forth_sem.at[1, i, o],
+            sending.at[o, :, pl.ds(low, count)],
+            arrived.at[o, :, pl.ds(low, count)],
+            send_sem.at[1],
+            forth_sem.at[0 if offsets[o] < 0 else 1],
             device_id={"patch": partner[o]},
+            device_id_type=MESH,
+        )
+
+    def all_back(i):
+        low, count = numbered[i]
+        return pltpu.make_async_remote_copy(
+            returning.at[:, :, pl.ds(low, count)],
+            arrived_back[i].at[:, pl.ds(0, most)],
+            send_sem.at[0],
+            back_sem.at[i],
+            device_id={"patch": source[0]},
+            device_id_type=MESH,
+        )
+
+    def all_forth(first, count, sem):
+        return pltpu.make_async_remote_copy(
+            sending.at[pl.ds(first, count)],
+            arrived.at[pl.ds(first, count)],
+            send_sem.at[1],
+            forth_sem.at[sem],
+            device_id={"patch": partner[0]},
             device_id_type=MESH,
         )
 
@@ -291,24 +315,27 @@
         first = len(chunks[0]) if c else 0
         return range(first, first + len(chunks[c]))
 
-    def sum_own(c):
-        low, count = parts[c]
-        left = side_by_side(smooth, tiles, low, count)
+    def sum_own():
+        left = side_by_side(smooth, tiles, 0, rows)
         for first in range(0, tiles, most):
             sums = gathered(left, first)
             for s in range(most):
-                own[first + s, pl.ds(low, count)] = sums[:, s * tile_len : (s + 1) * tile_len]
+                own[first + s] = sums[:, s * tile_len : (s + 1) * tile_len]
+
+    def await_entry(group, sem):
+        later = jnp.int32(0)
+        for o in group:
+            later = later + jnp.where(source[o] > me_p, 1, 0)
+
+        @pl.when(later > 0)
+        def _():
+            pl.semaphore_wait(enter_sem.at[sem], later)
 
     def send_back(c):
         for o in upper:
             sum_back(c, o)
         if c == 0:
-            for o in upper:
-
-                @pl.when(source[o] > me_p)
-                def _(o=o):
-                    pl.semaphore_wait(enter_sem.at[opposite[o]], 1)
-
+            await_entry(upper, 0)
         for i in indices(c):
             for o in upper:
                 copy_back(o, i).start()
@@ -322,7 +349,6 @@
                     copy_back(o, i).start()
 
     send_back(0)
-    sum_own(0)
 
     def unpack(side, base):
         for i in range(wide // 2):
@@ -358,27 +384,26 @@
         forward_pair(level)
 
     send_back(1)
+    await_entry(lower, 1)
     for o in lower:
 
         @pl.when(source[o] > me_p)
         def _(o=o):
-            pl.semaphore_wait(enter_sem.at[opposite[o]], 1)
             for i in range(len(numbered)):
                 copy_back(o, i).start()
 
-    sum_own(1)
+    sum_own()
 
     for i, (low, count) in enumerate(numbered):
-        for o in upper + lower:
-            copy_back(o, i).wait_recv()
+        all_back(i).wait_recv()
         for t in range(tiles):
             value = own[t, pl.ds(low, count)]
             for o in range(link_len):
-                value = value + arrived_back[i][o][slot_of[t, o]].astype(F32)
+                value = value + arrived_back[i][o, slot_of[t, o]].astype(F32)
             ext[t, pl.ds(low, count)] = value.astype(BF16)
         for o in lower + upper:
             for s in range(most):
-                sending[o][s, pl.ds(low, count)] = ext[send[0, s, o], pl.ds(low, count)]
+                sending[o, s, pl.ds(low, count)] = ext[send[0, s, o], pl.ds(low, count)]
             copy_forth(o, i).start()
 
     def spread(left, named, t):
@@ -405,11 +430,11 @@
     left = side_by_side(ext, tiles, 0, rows)
     for t in range(0, tiles, 2):
         put(t, spread(left, range(tiles), t), True)
-    for group in (upper, lower):
-        for i in range(len(numbered)):
-            for o in group:
-                copy_forth(o, i).wait_recv()
-        left = jnp.concatenate([side_by_side(arrived[o], most, 0, rows) for o in group], axis=1)
+    for first, group in ((0, upper), (link_len // 2, lower)):
+        all_forth(first, link_len // 2, first * 2 // link_len).wait_recv()
+        left = jnp.concatenate(
+            [side_by_side(arrived.at[o], most, 0, rows) for o in group], axis=1
+        )
         named = [tiles + o * most + s for o in group for s in range(most)]
         for t in range(0, tiles, 2):
             put(t, spread(left, named, t), False)
@@ -421,9 +446,8 @@
         result = jnp.dot(part, interp[t], preferred_element_type=F32)
         out[:, :, t * fine : (t + 1) * fine] = result.reshape(members, level_len, fine)
     for i in range(len(numbered)):
-        for o in range(link_len):
-            copy_back(o, i).wait_send()
-            copy_forth(o, i).wait_send()
+        all_back(i).wait_send()
+    all_forth(0, link_len, 0).wait_send()
 
     @pl.when(me_l > 0)
     def _():
@@ -452,7 +476,7 @@
         sizes = [count for part in chunks_of([(0, rows - edge), (rows - edge, edge)]) for _, count in part]
 
         def per_link(count, size=rows):
-            return [pltpu.VMEM((count, size, tile_len), BF16) for _ in range(link_len)]
+            return pltpu.VMEM((link_len, count, size, tile_len), BF16)
 
         return pl.pallas_call(
             functools.partial(kernel, n_patch, n_lev),
@@ -481,15 +505,14 @@
                 pltpu.SMEM((tiles, link_len), jnp.int32),
                 pltpu.SemaphoreType.DMA((6,)),
                 pltpu.SemaphoreType.DMA((4,)),
-                pltpu.SemaphoreType.DMA((2, len(sizes), link_len)),
-                pltpu.SemaphoreType.DMA((2, len(sizes), link_len)),
-                pltpu.SemaphoreType.REGULAR((link_len,)),
+                pltpu.SemaphoreType.DMA((2,)),
+                pltpu.SemaphoreType.DMA((len(sizes),)),
+                pltpu.SemaphoreType.DMA((2,)),
+                pltpu.SemaphoreType.REGULAR((2,)),
                 pltpu.SemaphoreType.REGULAR,
             ]
-            + per_link(most)
-            + per_link(most)
-            + per_link(most)
-            + [ref for size in sizes for ref in per_link(most + 1, size)],
+            + [per_link(most)] * 3
+            + [per_link(most + 1, size) for size in sizes],
             compiler_params=pltpu.CompilerParams(collective_id=0, has_side_effects=True),
         )(fields, interp, conv_weight, weight, send, tile_pattern)
 

time: 20.4 us -> 20.2 us (level)
  no operation moved by 1% of the time
where the time goes in v2:
time: 20.2 us; the launch traced here: 20 us
  Pallas kernels  19.1 us (95%)
  local copies, waits for them, and re-layouts  0.97 us (5%)
    pallas_call x1, Pallas kernels, shards(): pl.pallas_call(functools.partial(kernel, n_patch, n_lev), name='localize'...  19.1 us
    unnamed x1, local copies, waits for them, and re-layouts  0.97 us

profile of v2, /device:TPU:0, one launch (start us, length us, event | category | flops | bytes accessed | tf_op | source)
XLA Modules:
  0.0 20.0 jit_solution(2802861573957699568)
XLA Ops:
  0.0 19.1 %localize.1 = f32[8,16,2048]{2,1,0:T(8,128)S(1)} custom-call(bf16[8,16,2048]{2,1,0:T(8,128)(2,1)} %fields_hbm.1, bf16[8,128,256]{2,1,0:T(8,128)(2,1)} %interp_hbm.1, bf16[8,8,128,128]{3,2,1,0:T(8,128)(2,1)} %conv_hbm.1, f32[5,32]{1,0:T(8,128)} %bitcast.2, s32[1,2,4]{2,1,0:T(2,128)} %bitcast.3, s32[8,8]{1,0:T(8,128)} %pattern_hbm.1), custom_call_target="tpu_custom_call" | custom-call | tf_op jit(solution)/shard_map/localize/pallas_call | solution.py:481
  19.1 1.0 %copy.8 = f32[8,16,2048]{2,1,0:T(8,128)} copy(f32[8,16,2048]{2,1,0:T(8,128)S(1)} %localize.1) | data formatting | bytes 2097152

commit v3 on v2

--- a/solution.py
+++ b/solution.py
@@ -341,11 +341,15 @@
                 copy_back(o, i).start()
         for o in lower:
             sum_back(c, o)
-        for o in lower:
-
-            @pl.when(source[o] < me_p)
-            def _(o=o):
-                for i in indices(c):
+        for i in indices(c):
+            for o in lower:
+                if c == 0:
+
+                    @pl.when(source[o] < me_p)
+                    def _(o=o, i=i):
+                        copy_back(o, i).start()
+
+                else:
                     copy_back(o, i).start()
 
     send_back(0)
@@ -383,15 +387,15 @@
     for level in list(range(0, wide, 2)) + list(range(level_len - wide, level_len, 2)):
         forward_pair(level)
 
+    await_entry(lower, 1)
+    for i in indices(0):
+        for o in lower:
+
+            @pl.when(source[o] > me_p)
+            def _(o=o, i=i):
+                copy_back(o, i).start()
+
     send_back(1)
-    await_entry(lower, 1)
-    for o in lower:
-
-        @pl.when(source[o] > me_p)
-        def _(o=o):
-            for i in range(len(numbered)):
-                copy_back(o, i).start()
-
     sum_own()
 
     for i, (low, count) in enumerate(numbered):
@@ -427,6 +431,14 @@
                     value = value + mixed[t + i, pl.ds(place, count)]
                 mixed[t + i, pl.ds(place, count)] = value
 
+    def finish(first):
+        for t in (first, first + 1):
+            part = jnp.concatenate(
+                [mixed[t, pl.ds(m, level_len, stride=members), :] for m in range(members)], axis=0
+            ).astype(BF16)
+            result = jnp.dot(part, interp[t], preferred_element_type=F32)
+            out[:, :, t * fine : (t + 1) * fine] = result.reshape(members, level_len, fine)
+
     left = side_by_side(ext, tiles, 0, rows)
     for t in range(0, tiles, 2):
         put(t, spread(left, range(tiles), t), True)
@@ -438,13 +450,9 @@
         named = [tiles + o * most + s for o in group for s in range(most)]
         for t in range(0, tiles, 2):
             put(t, spread(left, named, t), False)
-
-    for t in range(tiles):
-        part = jnp.concatenate(
-            [mixed[t, pl.ds(m, level_len, stride=members), :] for m in range(members)], axis=0
-        ).astype(BF16)
-        result = jnp.dot(part, interp[t], preferred_element_type=F32)
-        out[:, :, t * fine : (t + 1) * fine] = result.reshape(members, level_len, fine)
+            if group is lower and t > 0:
+                finish(t - 2)
+    finish(tiles - 2)
     for i in range(len(numbered)):
         all_back(i).wait_send()
     all_forth(0, link_len, 0).wait_send()

time: 20.2 us -> 19.9 us (0.985)
  Pallas kernels: 19.1 us -> 18.7 us
    pallas_call x1, Pallas kernels: 19.1 us -> 18.7 us  [shards(): pl.pallas_call(functools.partial(kernel, n_patch, n_lev), name='localize'...]
where the time goes in v3:
time: 19.9 us; the launch traced here: 19.7 us
  Pallas kernels  18.7 us (94%)
  local copies, waits for them, and re-layouts  0.97 us (5%)
    pallas_call x1, Pallas kernels, shards(): pl.pallas_call(functools.partial(kernel, n_patch, n_lev), name='localize'...  18.7 us
    unnamed x1, local copies, waits for them, and re-layouts  0.97 us

profile of v3, /device:TPU:0, one launch (start us, length us, event | category | flops | bytes accessed | tf_op | source)
XLA Modules:
  0.0 19.7 jit_solution(7034564930537618966)
XLA Ops:
  0.0 18.7 %localize.1 = f32[8,16,2048]{2,1,0:T(8,128)S(1)} custom-call(bf16[8,16,2048]{2,1,0:T(8,128)(2,1)} %fields_hbm.1, bf16[8,128,256]{2,1,0:T(8,128)(2,1)} %interp_hbm.1, bf16[8,8,128,128]{3,2,1,0:T(8,128)(2,1)} %conv_hbm.1, f32[5,32]{1,0:T(8,128)} %bitcast.2, s32[1,2,4]{2,1,0:T(2,128)} %bitcast.3, s32[8,8]{1,0:T(8,128)} %pattern_hbm.1), custom_call_target="tpu_custom_call" | custom-call | tf_op jit(solution)/shard_map/localize/pallas_call | solution.py:489
  18.7 1.0 %copy.8 = f32[8,16,2048]{2,1,0:T(8,128)} copy(f32[8,16,2048]{2,1,0:T(8,128)S(1)} %localize.1) | data formatting | bytes 2097152

commit v4 on v3

--- a/solution.py
+++ b/solution.py
@@ -47,6 +47,7 @@
     fields,
     interp,
     conv,
+    turned,
     coarse,
     levels,
     middle,
@@ -87,6 +88,14 @@
     me_p, me_l = lax.axis_index("patch"), lax.axis_index("lev")
     partner = [lax.rem(me_p + d + n_patch, n_patch) for d in offsets]
     source = [lax.rem(me_p - d + n_patch, n_patch) for d in offsets]
+
+    def rank(index):
+        return jnp.where(index < n_patch - 4, index, 2 * n_patch - 5 - index)
+
+    me_rank = rank(me_p)
+    ahead = [rank(other) < me_rank for other in partner]
+    behind = [rank(other) > me_rank for other in partner]
+    answers = [rank(other) > me_rank for other in source]
     upper = sorted((o for o in range(link_len) if offsets[o] < 0), key=lambda o: offsets[o])
     lower = sorted((o for o in range(link_len) if offsets[o] > 0), key=lambda o: -offsets[o])
 
@@ -106,7 +115,7 @@
     barrier = pltpu.get_barrier_semaphore()
     for o in range(link_len):
 
-        @pl.when(partner[o] > me_p)
+        @pl.when(behind[o])
         def _(o=o):
             pl.semaphore_signal(
                 barrier, inc=1, device_id={"patch": partner[o]}, device_id_type=MESH
@@ -132,7 +141,7 @@
     ext[tiles] = jnp.zeros((rows, tile_len), BF16)
     before = jnp.where(me_l > 0, 1, 0)
     for o in range(link_len):
-        before = before + jnp.where(partner[o] < me_p, 1, 0)
+        before = before + jnp.where(ahead[o], 1, 0)
 
     @pl.when(before > 0)
     def _():
@@ -140,10 +149,11 @@
 
     for o in range(link_len):
 
-        @pl.when(partner[o] < me_p)
+        @pl.when(ahead[o])
         def _(o=o):
+            wrapped = partner[o] < me_p if offsets[o] > 0 else partner[o] > me_p
             pl.semaphore_signal(
-                enter_sem.at[0 if offsets[o] < 0 else 1],
+                enter_sem.at[jnp.where(wrapped, 1, 0)],
                 inc=1,
                 device_id={"patch": partner[o]},
                 device_id_type=MESH,
@@ -153,11 +163,61 @@
     def _():
         pl.semaphore_signal(enter_lev, inc=1, device_id={"lev": me_l - 1}, device_id_type=MESH)
 
+    load_f.wait()
+    load_i.wait()
+    down = []
+    split = tiles // 2
+    for h in range(2):
+        for t in range(h * split, (h + 1) * split):
+            block = fields[:, :, t * fine : (t + 1) * fine].reshape(rows, fine)
+            coarse[t] = dot_t(block, interp[t])
+            for l in range(level_len):
+                levels[wide + l, t] = coarse[t, pl.ds(l, members, stride=level_len), :]
+        some = pl.ds(h * split, split)
+        for i in range(wide // 2):
+            low = [levels[wide + 2 * i + n, some] for n in range(2)]
+            high = [levels[level_len + 2 * i + n, some] for n in range(2)]
+            halo_out[0, i, some] = jnp.concatenate(low, axis=1).astype(BF16)
+            halo_out[1, i, some] = jnp.concatenate(high, axis=1).astype(BF16)
+        down.append(
+            pltpu.make_async_remote_copy(
+                halo_out.at[0, :, some],
+                halo_in.at[1, :, some],
+                halo_sem.at[0],
+                halo_sem.at[1],
+                device_id={"lev": lax.rem(me_l + n_lev - 1, n_lev)},
+                device_id_type=MESH,
+            )
+        )
+        @pl.when(me_l > 0)
+        def _(h=h):
+            down[h].start()
+
+    all_down = pltpu.make_async_remote_copy(
+        halo_out.at[0],
+        halo_in.at[1],
+        halo_sem.at[0],
+        halo_sem.at[1],
+        device_id={"lev": lax.rem(me_l + n_lev - 1, n_lev)},
+        device_id_type=MESH,
+    )
+    all_up = pltpu.make_async_remote_copy(
+        halo_out.at[1],
+        halo_in.at[0],
+        halo_sem.at[2],
+        halo_sem.at[3],
+        device_id={"lev": lax.rem(me_l + 1, n_lev)},
+        device_id_type=MESH,
+    )
+
+    @pl.when(me_l < n_lev - 1)
+    def _():
+        pl.semaphore_wait(enter_lev, 1)
+        all_up.start()
+
     load_p.wait()
     load_s.wait()
     load_w.wait()
-    load_f.wait()
-    load_i.wait()
     empty = sum(k_len << (bits * i) for i in range(per_word))
     for t in range(tiles):
         packed = [jnp.int32(empty) for _ in range(words)]
@@ -173,44 +233,6 @@
             for s in range(most):
                 index = jnp.where(send[0, s, o] == t, s, index)
             slot_of[t, o] = index
-    for t in range(tiles):
-        block = fields[:, :, t * fine : (t + 1) * fine].reshape(rows, fine)
-        coarse[t] = dot_t(block, interp[t])
-        for l in range(level_len):
-            levels[wide + l, t] = coarse[t, pl.ds(l, members, stride=level_len), :]
-    for i in range(wide // 2):
-        low = jnp.concatenate([levels[wide + 2 * i], levels[wide + 2 * i + 1]], axis=1)
-        top = level_len + 2 * i
-        high = jnp.concatenate([levels[top], levels[top + 1]], axis=1)
-        halo_out[0, i] = low.astype(BF16)
-        halo_out[1, i] = high.astype(BF16)
-
-    down = pltpu.make_async_remote_copy(
-        halo_out.at[0],
-        halo_in.at[1],
-        halo_sem.at[0],
-        halo_sem.at[1],
-        device_id={"lev": lax.rem(me_l + n_lev - 1, n_lev)},
-        device_id_type=MESH,
-    )
-    up = pltpu.make_async_remote_copy(
-        halo_out.at[1],
-        halo_in.at[0],
-        halo_sem.at[2],
-        halo_sem.at[3],
-        device_id={"lev": lax.rem(me_l + 1, n_lev)},
-        device_id_type=MESH,
-    )
-
-    @pl.when(me_l > 0)
-    def _():
-        down.start()
-
-    @pl.when(me_l < n_lev - 1)
-    def _():
-        pl.semaphore_wait(enter_lev, 1)
-        up.start()
-
     start = me_l * level_len
 
     def coefficient(level, column):
@@ -258,13 +280,23 @@
         )
         return dot_t(left, right)
 
+    def gathered_turned(left, first):
+        right = jnp.concatenate(
+            [
+                jnp.concatenate([turned[t, which[t, first + s]] for t in range(tiles)], axis=0)
+                for s in range(most)
+            ],
+            axis=1,
+        )
+        return jnp.dot(left, right, preferred_element_type=F32)
+
     def side_by_side(ref, count, low, size):
         return jnp.concatenate([ref[i, pl.ds(low, size)] for i in range(count)], axis=1)
 
     def sum_back(c, o):
         low, count = parts[c]
         left = side_by_side(smooth, tiles, low, count)
-        sums = gathered(left, tiles + o * most).astype(BF16)
+        sums = (gathered_turned if c else gathered)(left, tiles + o * most).astype(BF16)
         for s in range(most):
             returning[o, s, pl.ds(low, count)] = sums[:, s * tile_len : (s + 1) * tile_len]
 
@@ -318,24 +350,26 @@
     def sum_own():
         left = side_by_side(smooth, tiles, 0, rows)
         for first in range(0, tiles, most):
-            sums = gathered(left, first)
+            sums = gathered_turned(left, first)
             for s in range(most):
                 own[first + s] = sums[:, s * tile_len : (s + 1) * tile_len]
 
-    def await_entry(group, sem):
+    def await_entry(group, wrapped):
         later = jnp.int32(0)
         for o in group:
-            later = later + jnp.where(source[o] > me_p, 1, 0)
+            around = source[o] > me_p if offsets[o] > 0 else source[o] < me_p
+            wanted = jnp.logical_and(answers[o], around == wrapped)
+            later = later + jnp.where(wanted, 1, 0)
 
         @pl.when(later > 0)
         def _():
-            pl.semaphore_wait(enter_sem.at[sem], later)
+            pl.semaphore_wait(enter_sem.at[1 if wrapped else 0], later)
 
     def send_back(c):
         for o in upper:
             sum_back(c, o)
         if c == 0:
-            await_entry(upper, 0)
+            await_entry(upper + lower, False)
         for i in indices(c):
             for o in upper:
                 copy_back(o, i).start()
@@ -353,6 +387,9 @@
                     copy_back(o, i).start()
 
     send_back(0)
+    for t in range(tiles):
+        for k in range(k_len + 1):
+            turned[t, k] = conv[t, k].T
 
     def unpack(side, base):
         for i in range(wide // 2):
@@ -364,9 +401,17 @@
         for i in range(wide):
             levels[base + i] = jnp.zeros(levels.shape[1:], F32)
 
+    await_entry(upper + lower, True)
+    for i in indices(0):
+        for o in lower:
+
+            @pl.when(source[o] > me_p)
+            def _(o=o, i=i):
+                copy_back(o, i).start()
+
     @pl.when(me_l > 0)
     def _():
-        up.wait_recv()
+        all_up.wait_recv()
         unpack(0, 0)
 
     @pl.when(me_l == 0)
@@ -375,7 +420,7 @@
 
     @pl.when(me_l < n_lev - 1)
     def _():
-        down.wait_recv()
+        all_down.wait_recv()
         unpack(1, wide + level_len)
 
     @pl.when(me_l == n_lev - 1)
@@ -386,14 +431,6 @@
         adjoint_level(level)
     for level in list(range(0, wide, 2)) + list(range(level_len - wide, level_len, 2)):
         forward_pair(level)
-
-    await_entry(lower, 1)
-    for i in indices(0):
-        for o in lower:
-
-            @pl.when(source[o] > me_p)
-            def _(o=o, i=i):
-                copy_back(o, i).start()
 
     send_back(1)
     sum_own()
@@ -408,7 +445,20 @@
         for o in lower + upper:
             for s in range(most):
                 sending[o, s, pl.ds(low, count)] = ext[send[0, s, o], pl.ds(low, count)]
+        for o in lower:
+
+            @pl.when(partner[o] < me_p)
+            def _(o=o, i=i):
+                copy_forth(o, i).start()
+
+        for o in upper:
             copy_forth(o, i).start()
+        for o in lower:
+
+            @pl.when(partner[o] > me_p)
+            def _(o=o, i=i):
+                copy_forth(o, i).start()
+
 
     def spread(left, named, t):
         right = jnp.concatenate(
@@ -459,11 +509,11 @@
 
     @pl.when(me_l > 0)
     def _():
-        down.wait_send()
+        all_down.wait_send()
 
     @pl.when(me_l < n_lev - 1)
     def _():
-        up.wait_send()
+        all_up.wait_send()
 
 
 def solution(mesh):
@@ -498,6 +548,7 @@
                 pltpu.SMEM(tile_pattern.shape, jnp.int32),
                 pltpu.VMEM(fields.shape, BF16),
                 pltpu.VMEM(interp.shape, BF16),
+                pltpu.VMEM((tiles, k_len + 1, tile_len, tile_len), BF16),
                 pltpu.VMEM((tiles, k_len + 1, tile_len, tile_len), BF16),
                 pltpu.VMEM((tiles, rows, tile_len), F32),
                 pltpu.VMEM((level_len + 2 * wide, tiles, members, tile_len), F32),

time: 19.9 us -> 19.7 us (0.990)
  no operation moved by 1% of the time
where the time goes in v4:
time: 19.7 us; the launch traced here: 19.6 us
  Pallas kernels  18.6 us (94%)
  local copies, waits for them, and re-layouts  0.97 us (5%)
    pallas_call x1, Pallas kernels, shards(): pl.pallas_call(functools.partial(kernel, n_patch, n_lev), name='localize'...  18.6 us
    unnamed x1, local copies, waits for them, and re-layouts  0.97 us

profile of v4, /device:TPU:0, one launch (start us, length us, event | category | flops | bytes accessed | tf_op | source)
XLA Modules:
  0.0 19.6 jit_solution(14610462716097339674)
XLA Ops:
  0.0 18.6 %localize.1 = f32[8,16,2048]{2,1,0:T(8,128)S(1)} custom-call(bf16[8,16,2048]{2,1,0:T(8,128)(2,1)} %fields_hbm.1, bf16[8,128,256]{2,1,0:T(8,128)(2,1)} %interp_hbm.1, bf16[8,8,128,128]{3,2,1,0:T(8,128)(2,1)} %conv_hbm.1, f32[5,32]{1,0:T(8,128)} %bitcast.2, s32[1,2,4]{2,1,0:T(2,128)} %bitcast.3, s32[8,8]{1,0:T(8,128)} %pattern_hbm.1), custom_call_target="tpu_custom_call" | custom-call | tf_op jit(solution)/shard_map/localize/pallas_call | solution.py:539
  18.6 1.0 %copy.8 = f32[8,16,2048]{2,1,0:T(8,128)} copy(f32[8,16,2048]{2,1,0:T(8,128)S(1)} %localize.1) | data formatting | bytes 2097152

commit v5 on v4

--- a/solution.py
+++ b/solution.py
@@ -40,7 +40,9 @@
     weight_hbm,
     send_hbm,
     pattern_hbm,
-    out,
+    left_out,
+    turn_out,
+    base_out,
     weight,
     send,
     pattern,
@@ -139,32 +141,54 @@
         for o in range(link_len):
             arrived_back[i][o, most] = jnp.zeros((count, tile_len), BF16)
     ext[tiles] = jnp.zeros((rows, tile_len), BF16)
-    before = jnp.where(me_l > 0, 1, 0)
-    for o in range(link_len):
-        before = before + jnp.where(ahead[o], 1, 0)
-
-    @pl.when(before > 0)
-    def _():
-        pl.semaphore_wait(barrier, before)
-
-    for o in range(link_len):
-
-        @pl.when(ahead[o])
-        def _(o=o):
-            wrapped = partner[o] < me_p if offsets[o] > 0 else partner[o] > me_p
-            pl.semaphore_signal(
-                enter_sem.at[jnp.where(wrapped, 1, 0)],
-                inc=1,
-                device_id={"patch": partner[o]},
-                device_id_type=MESH,
-            )
-
-    @pl.when(me_l > 0)
-    def _():
-        pl.semaphore_signal(enter_lev, inc=1, device_id={"lev": me_l - 1}, device_id_type=MESH)
-
+    eager = jnp.logical_or(me_p < n_patch - 4, me_p >= n_patch - 2)
+
+    def enter():
+        before = jnp.where(me_l > 0, 1, 0)
+        for o in range(link_len):
+            before = before + jnp.where(ahead[o], 1, 0)
+
+        @pl.when(before > 0)
+        def _():
+            pl.semaphore_wait(barrier, before)
+
+        for o in range(link_len):
+
+            @pl.when(ahead[o])
+            def _(o=o):
+                wrapped = partner[o] < me_p if offsets[o] > 0 else partner[o] > me_p
+                pl.semaphore_signal(
+                    enter_sem.at[jnp.where(wrapped, 1, 0)],
+                    inc=1,
+                    device_id={"patch": partner[o]},
+                    device_id_type=MESH,
+                )
+
+        @pl.when(me_l > 0)
+        def _():
+            pl.semaphore_signal(enter_lev, inc=1, device_id={"lev": me_l - 1}, device_id_type=MESH)
+
+    pl.when(eager)(enter)
     load_f.wait()
     load_i.wait()
+    load_p.wait()
+    load_s.wait()
+    load_w.wait()
+    empty = sum(k_len << (bits * i) for i in range(per_word))
+    for t in range(tiles):
+        packed = [jnp.int32(empty) for _ in range(words)]
+        for k in range(k_len):
+            named = pattern[t, k]
+            for w in range(words):
+                packed[w] = packed[w] + jnp.int32(k - k_len) * power[w, named]
+        for e in range(entries):
+            w, place = e // per_word, bits * (e % per_word)
+            which[t, e] = (packed[w] >> place) & ((1 << bits) - 1)
+        for o in range(link_len):
+            index = jnp.int32(most)
+            for s in range(most):
+                index = jnp.where(send[0, s, o] == t, s, index)
+            slot_of[t, o] = index
     down = []
     split = tiles // 2
     for h in range(2):
@@ -189,6 +213,9 @@
                 device_id_type=MESH,
             )
         )
+        if h == 0:
+            pl.when(jnp.logical_not(eager))(enter)
+
         @pl.when(me_l > 0)
         def _(h=h):
             down[h].start()
@@ -210,29 +237,6 @@
         device_id_type=MESH,
     )
 
-    @pl.when(me_l < n_lev - 1)
-    def _():
-        pl.semaphore_wait(enter_lev, 1)
-        all_up.start()
-
-    load_p.wait()
-    load_s.wait()
-    load_w.wait()
-    empty = sum(k_len << (bits * i) for i in range(per_word))
-    for t in range(tiles):
-        packed = [jnp.int32(empty) for _ in range(words)]
-        for k in range(k_len):
-            named = pattern[t, k]
-            for w in range(words):
-                packed[w] = packed[w] + jnp.int32(k - k_len) * power[w, named]
-        for e in range(entries):
-            w, place = e // per_word, bits * (e % per_word)
-            which[t, e] = (packed[w] >> place) & ((1 << bits) - 1)
-        for o in range(link_len):
-            index = jnp.int32(most)
-            for s in range(most):
-                index = jnp.where(send[0, s, o] == t, s, index)
-            slot_of[t, o] = index
     start = me_l * level_len
 
     def coefficient(level, column):
@@ -373,6 +377,13 @@
         for i in indices(c):
             for o in upper:
                 copy_back(o, i).start()
+        if c == 0:
+
+            @pl.when(me_l < n_lev - 1)
+            def _():
+                pl.semaphore_wait(enter_lev, 1)
+                all_up.start()
+
         for o in lower:
             sum_back(c, o)
         for i in indices(c):
@@ -470,39 +481,31 @@
         )
         return jnp.dot(left, right, preferred_element_type=F32)
 
-    def places():
-        return [(0, parts[0][1], edge), (parts[1][0], edge, 0), (parts[1][0] + edge, edge, rows - edge)]
-
-    def put(t, sums, fresh):
-        for begin, count, place in places():
+    def add(left, named, fresh):
+        for t in range(0, tiles, 2):
+            sums = spread(left, named, t)
             for i in range(2):
-                value = sums[begin : begin + count, i * tile_len : (i + 1) * tile_len]
-                if not fresh:
-                    value = value + mixed[t + i, pl.ds(place, count)]
-                mixed[t + i, pl.ds(place, count)] = value
-
-    def finish(first):
-        for t in (first, first + 1):
-            part = jnp.concatenate(
-                [mixed[t, pl.ds(m, level_len, stride=members), :] for m in range(members)], axis=0
-            ).astype(BF16)
-            result = jnp.dot(part, interp[t], preferred_element_type=F32)
-            out[:, :, t * fine : (t + 1) * fine] = result.reshape(members, level_len, fine)
-
-    left = side_by_side(ext, tiles, 0, rows)
-    for t in range(0, tiles, 2):
-        put(t, spread(left, range(tiles), t), True)
-    for first, group in ((0, upper), (link_len // 2, lower)):
-        all_forth(first, link_len // 2, first * 2 // link_len).wait_recv()
-        left = jnp.concatenate(
+                value = sums[:, i * tile_len : (i + 1) * tile_len]
+                mixed[t + i] = value if fresh else value + mixed[t + i]
+
+    def received(group):
+        return jnp.concatenate(
             [side_by_side(arrived.at[o], most, 0, rows) for o in group], axis=1
         )
-        named = [tiles + o * most + s for o in group for s in range(most)]
-        for t in range(0, tiles, 2):
-            put(t, spread(left, named, t), False)
-            if group is lower and t > 0:
-                finish(t - 2)
-    finish(tiles - 2)
+
+    def entries_of(group):
+        return [tiles + o * most + s for o in group for s in range(most)]
+
+    add(side_by_side(ext, tiles, 0, rows), range(tiles), True)
+    for t in range(tiles):
+        stack = jnp.concatenate([conv[t, which[t, e]] for e in entries_of(lower)], axis=0)
+        turn_out[t] = jnp.dot(stack, interp[t], preferred_element_type=F32).astype(BF16)
+    all_forth(0, link_len // 2, 0).wait_recv()
+    add(received(upper), entries_of(upper), False)
+    for t in range(tiles):
+        base_out[t] = jnp.dot(mixed[t].astype(BF16), interp[t], preferred_element_type=F32)
+    all_forth(link_len // 2, link_len // 2, 1).wait_recv()
+    left_out[...] = received(lower)
     for i in range(len(numbered)):
         all_back(i).wait_send()
     all_forth(0, link_len, 0).wait_send()
@@ -514,6 +517,22 @@
     @pl.when(me_l < n_lev - 1)
     def _():
         all_up.wait_send()
+
+
+def finish(places, left, turn, base, out_hbm, out, sem):
+    tiles, _, fine = turn.shape
+    level_len = out.shape[1]
+    copies = []
+    for t in range(tiles):
+        sums = base[t] + jnp.dot(left[...], turn[t], preferred_element_type=F32)
+        columns = pl.ds(t * fine, fine)
+        for row, level in places:
+            out[:, level, columns] = sums[row : row + out.shape[0]]
+        copy = pltpu.make_async_copy(out.at[:, :, columns], out_hbm.at[:, :, columns], sem.at[t])
+        copy.start()
+        copies.append(copy)
+    for copy in copies:
+        copy.wait()
 
 
 def solution(mesh):
@@ -536,12 +555,22 @@
         def per_link(count, size=rows):
             return pltpu.VMEM((link_len, count, size, tile_len), BF16)
 
-        return pl.pallas_call(
+        vmem_spec = pl.BlockSpec(memory_space=pltpu.VMEM)
+        half_len = link_len // 2 * most * tile_len
+        order = list(range(wide, level_len - wide))
+        order += list(range(wide)) + list(range(level_len - wide, level_len))
+        places = [(i * members, level) for i, level in enumerate(order)]
+
+        left, turn, base = pl.pallas_call(
             functools.partial(kernel, n_patch, n_lev),
             name="localize",
-            out_shape=pltpu.VMEM(fields.shape, F32),
+            out_shape=[
+                pltpu.VMEM((rows, half_len), BF16),
+                pltpu.VMEM((tiles, half_len, fine), BF16),
+                pltpu.VMEM((tiles, rows, fine), F32),
+            ],
             in_specs=[any_spec] * 6,
-            out_specs=pl.BlockSpec(memory_space=pltpu.VMEM),
+            out_specs=[vmem_spec] * 3,
             scratch_shapes=[
                 pltpu.SMEM(weight.shape, F32),
                 pltpu.SMEM(send.shape, jnp.int32),
@@ -574,6 +603,18 @@
             + [per_link(most + 1, size) for size in sizes],
             compiler_params=pltpu.CompilerParams(collective_id=0, has_side_effects=True),
         )(fields, interp, conv_weight, weight, send, tile_pattern)
+        return pl.pallas_call(
+            functools.partial(finish, places),
+            name="finish",
+            out_shape=jax.ShapeDtypeStruct(fields.shape, F32),
+            in_specs=[vmem_spec] * 3,
+            out_specs=any_spec,
+            scratch_shapes=[
+                pltpu.VMEM(fields.shape, F32),
+                pltpu.SemaphoreType.DMA((tiles,)),
+            ],
+            compiler_params=pltpu.CompilerParams(vmem_limit_bytes=8 << 20),
+        )(left, turn, base)
 
     in_specs = (
         P(None, "lev", "patch"),

time: 19.7 us -> 19.2 us (0.975)
  local copies, waits for them, and re-layouts: 0.97 us -> 0 us
  Pallas kernels: 18.6 us -> 19.1 us
    pallas_call x0 -> x1, Pallas kernels: none -> 1.43 us  [shards(): pl.pallas_call(functools.partial(finish, places), name='finish', out_shap...]
    unnamed x1 -> x0, local copies, waits for them, and re-layouts: 0.97 us -> none
    pallas_call x1, Pallas kernels: 18.6 us -> 17.6 us  [shards(): pl.pallas_call(functools.partial(kernel, n_patch, n_lev), name='localize'...]
where the time goes in v5:
time: 19.2 us; the launch traced here: 19.1 us
  Pallas kernels  19.1 us (99%)
    pallas_call x1, Pallas kernels, shards(): pl.pallas_call(functools.partial(kernel, n_patch, n_lev), name='localize'...  17.6 us
    pallas_call x1, Pallas kernels, shards(): pl.pallas_call(functools.partial(finish, places), name='finish', out_shap...  1.43 us

profile of v5, /device:TPU:0, one launch (start us, length us, event | category | flops | bytes accessed | tf_op | source)
XLA Modules:
  0.0 19.1 jit_solution(10852035687927593118)
XLA Ops:
  0.0 17.6 %localize.1 = (bf16[128,512]{1,0:T(8,128)(2,1)S(1)}, bf16[8,512,256]{2,1,0:T(8,128)(2,1)S(1)}, f32[8,128,256]{2,1,0:T(8,128)S(1)}) custom-call(bf16[8,16,2048]{2,1,0:T(8,128)(2,1)} %fields_hbm.1, bf16[8,128,256]{2,1,0:T(8,128)(2,1)} %interp_hbm.1, bf16[8,8,128,128]{3,2,1,0:T(8,128)(2,1)} %conv_hbm.1, f32[5,32]{1,0:T(8,128)} %bitcast.2, s32[1,2,4]{2,1,0:T(2,128)} %bitcast.3, ...), custom_call_target="tpu_custom_call" | custom-call | tf_op jit(solution)/shard_map/localize/pallas_call | solution.py:564
  17.7 1.4 %finish.1 = f32[8,16,2048]{2,1,0:T(8,128)} custom-call(bf16[128,512]{1,0:T(8,128)(2,1)S(1)} %get-tuple-element.8.left, bf16[8,512,256]{2,1,0:T(8,128)(2,1)S(1)} %get-tuple-element.9.turn, f32[8,128,256]{2,1,0:T(8,128)S(1)} %get-tuple-element.10.base), custom_call_target="tpu_custom_call" | custom-call | tf_op jit(solution)/shard_map/finish/pallas_call | solution.py:606

commit v6 on v5

--- a/solution.py
+++ b/solution.py
@@ -22,9 +22,14 @@
 def chunks_of(parts):
     chunks = []
     for low, count in parts:
-        step = count // 2 if count % 32 == 0 else count
+        step = 32 if count % 32 == 0 else count
         chunks.append([(low + at, step) for at in range(0, count, step)])
     return chunks
+
+
+def split_rows(n_lev, level_len, members, wide):
+    early = level_len - wide if n_lev == 2 else level_len - 2 * wide
+    return [(0, early * members), (early * members, (level_len - early) * members)]
 
 
 def dot_t(left, right):
@@ -83,13 +88,22 @@
     rows = members * level_len
     total_levels = weight.shape[1]
     offsets = link_offsets(link_len // 2)
-    edge = wide * members
-    parts = [(0, rows - 2 * edge), (rows - 2 * edge, 2 * edge)]
+    two = n_lev == 2
+    parts = split_rows(n_lev, level_len, members, wide)
     chunks = chunks_of(parts)
     numbered = [(low, count) for part in chunks for low, count in part]
     me_p, me_l = lax.axis_index("patch"), lax.axis_index("lev")
     partner = [lax.rem(me_p + d + n_patch, n_patch) for d in offsets]
     source = [lax.rem(me_p - d + n_patch, n_patch) for d in offsets]
+
+    order = list(range(wide, level_len - wide))
+    order += list(range(wide)) + list(range(level_len - wide, level_len))
+
+    def turned_level(index):
+        return jnp.where(me_l == 0, index, level_len - 1 - index) if two else index
+
+    def level_of(group):
+        return turned_level(group) if two else order[group]
 
     def rank(index):
         return jnp.where(index < n_patch - 4, index, 2 * n_patch - 5 - index)
@@ -189,87 +203,89 @@
             for s in range(most):
                 index = jnp.where(send[0, s, o] == t, s, index)
             slot_of[t, o] = index
-    down = []
     split = tiles // 2
+    below = {"lev": lax.rem(me_l + n_lev - 1, n_lev)}
+    above = {"lev": lax.rem(me_l + 1, n_lev)}
+
+    def exchange(side, place, to, some=slice(None)):
+        return pltpu.make_async_remote_copy(
+            halo_out.at[side, :, some],
+            halo_in.at[place, :, some],
+            halo_sem.at[2 * side],
+            halo_sem.at[2 * side + 1],
+            device_id=to,
+            device_id_type=MESH,
+        )
+
+    down = exchange(0, 1, below)
+    up = down if two else exchange(1, 0, above)
     for h in range(2):
         for t in range(h * split, (h + 1) * split):
             block = fields[:, :, t * fine : (t + 1) * fine].reshape(rows, fine)
             coarse[t] = dot_t(block, interp[t])
             for l in range(level_len):
-                levels[wide + l, t] = coarse[t, pl.ds(l, members, stride=level_len), :]
+                place = pl.ds(turned_level(l), members, stride=level_len)
+                levels[wide + l, t] = coarse[t, place, :]
         some = pl.ds(h * split, split)
         for i in range(wide // 2):
-            low = [levels[wide + 2 * i + n, some] for n in range(2)]
-            high = [levels[level_len + 2 * i + n, some] for n in range(2)]
+            low = [level_len - 1 - 2 * i - n if two else 2 * i + n for n in range(2)]
+            low = [levels[wide + l, some] for l in low]
             halo_out[0, i, some] = jnp.concatenate(low, axis=1).astype(BF16)
-            halo_out[1, i, some] = jnp.concatenate(high, axis=1).astype(BF16)
-        down.append(
-            pltpu.make_async_remote_copy(
-                halo_out.at[0, :, some],
-                halo_in.at[1, :, some],
-                halo_sem.at[0],
-                halo_sem.at[1],
-                device_id={"lev": lax.rem(me_l + n_lev - 1, n_lev)},
-                device_id_type=MESH,
-            )
-        )
+            if not two:
+                high = [levels[level_len + 2 * i + n, some] for n in range(2)]
+                halo_out[1, i, some] = jnp.concatenate(high, axis=1).astype(BF16)
         if h == 0:
             pl.when(jnp.logical_not(eager))(enter)
 
         @pl.when(me_l > 0)
-        def _(h=h):
-            down[h].start()
-
-    all_down = pltpu.make_async_remote_copy(
-        halo_out.at[0],
-        halo_in.at[1],
-        halo_sem.at[0],
-        halo_sem.at[1],
-        device_id={"lev": lax.rem(me_l + n_lev - 1, n_lev)},
-        device_id_type=MESH,
-    )
-    all_up = pltpu.make_async_remote_copy(
-        halo_out.at[1],
-        halo_in.at[0],
-        halo_sem.at[2],
-        halo_sem.at[3],
-        device_id={"lev": lax.rem(me_l + 1, n_lev)},
-        device_id_type=MESH,
-    )
+        def _(some=some):
+            exchange(0, 1, below, some).start()
 
     start = me_l * level_len
 
-    def coefficient(level, column):
-        return weight[column, jnp.clip(start + level, 0, total_levels - 1)]
+    sign = jnp.where(me_l == 0, 1, -1) if two else 1
+
+    def coefficient(level, shift):
+        return weight[half + sign * shift, jnp.clip(start + turned_level(level), 0, total_levels - 1)]
 
     def adjoint_level(level):
-        value = coefficient(level - half, wide) * levels[wide + level - half]
+        value = coefficient(level - half, half) * levels[wide + level - half]
         for e in range(1 - half, half + 1):
-            value = value + coefficient(level + e, half - e) * levels[wide + level + e]
+            value = value + coefficient(level + e, -e) * levels[wide + level + e]
         if level < 0:
             value = jnp.where(start + level >= 0, value, 0.0)
         if level >= level_len:
-            value = jnp.where(start + level < total_levels, value, 0.0)
+            value = jnp.where(start + level < total_levels, value, 0.0) if not two else value
         middle[half + level] = value
 
     def forward_pair(level):
         both = []
         for l in (level, level + 1):
-            value = coefficient(l, 0) * middle[l]
+            value = coefficient(l, -half) * middle[l]
             for j in range(1, wide + 1):
-                value = value + coefficient(l, j) * middle[l + j]
+                value = value + coefficient(l, j - half) * middle[l + j]
             both.append(value)
         pair = jnp.concatenate(both, axis=1).astype(BF16)
-        if wide <= level < level_len - wide:
-            place = (level - wide) * members
-        else:
-            place = level if level < wide else level - level_len + 2 * wide
-            place = parts[1][0] + place * members
+        place = (level if two else order.index(level)) * members
         smooth[:, pl.ds(place, 2 * members), :] = pair
 
-    for level in range(half, level_len - half):
+    def clear(base):
+        for i in range(wide):
+            levels[base + i] = jnp.zeros(levels.shape[1:], F32)
+
+    if two:
+        clear(0)
+        for i in range(half):
+            middle[i] = jnp.zeros(middle.shape[1:], F32)
+        early = [range(level_len - half), range(0, level_len - wide, 2)]
+        late = [range(level_len - half, level_len + half), range(level_len - wide, level_len, 2)]
+    else:
+        early = [range(half, level_len - half), range(wide, level_len - wide, 2)]
+        late = [list(range(-half, half)) + list(range(level_len - half, level_len + half))]
+        late.append(list(range(0, wide, 2)) + list(range(level_len - wide, level_len, 2)))
+    for level in early[0]:
         adjoint_level(level)
-    for level in range(wide, level_len - wide, 2):
+    for level in early[1]:
         forward_pair(level)
 
     load_c.wait()
@@ -382,7 +398,7 @@
             @pl.when(me_l < n_lev - 1)
             def _():
                 pl.semaphore_wait(enter_lev, 1)
-                all_up.start()
+                up.start()
 
         for o in lower:
             sum_back(c, o)
@@ -408,10 +424,6 @@
             levels[base + 2 * i] = pair[:, :members]
             levels[base + 2 * i + 1] = pair[:, members:]
 
-    def clear(base):
-        for i in range(wide):
-            levels[base + i] = jnp.zeros(levels.shape[1:], F32)
-
     await_entry(upper + lower, True)
     for i in indices(0):
         for o in lower:
@@ -420,31 +432,48 @@
             def _(o=o, i=i):
                 copy_back(o, i).start()
 
-    @pl.when(me_l > 0)
-    def _():
-        all_up.wait_recv()
-        unpack(0, 0)
-
-    @pl.when(me_l == 0)
-    def _():
-        clear(0)
-
-    @pl.when(me_l < n_lev - 1)
-    def _():
-        all_down.wait_recv()
+    if two:
+        down.wait_recv()
         unpack(1, wide + level_len)
-
-    @pl.when(me_l == n_lev - 1)
-    def _():
-        clear(wide + level_len)
-
-    for level in list(range(-half, half)) + list(range(level_len - half, level_len + half)):
+    else:
+
+        @pl.when(me_l > 0)
+        def _():
+            up.wait_recv()
+            unpack(0, 0)
+
+        @pl.when(me_l == 0)
+        def _():
+            clear(0)
+
+        @pl.when(me_l < n_lev - 1)
+        def _():
+            down.wait_recv()
+            unpack(1, wide + level_len)
+
+        @pl.when(me_l == n_lev - 1)
+        def _():
+            clear(wide + level_len)
+
+    for level in late[0]:
         adjoint_level(level)
-    for level in list(range(0, wide, 2)) + list(range(level_len - wide, level_len, 2)):
+    for level in late[1]:
         forward_pair(level)
 
     send_back(1)
     sum_own()
+
+    last = len(numbered) - 1
+    around = me_p >= n_patch - max(offsets)
+
+    def near_forth(i):
+        for o in upper:
+            copy_forth(o, i).start()
+        for o in lower:
+
+            @pl.when(partner[o] > me_p)
+            def _(o=o):
+                copy_forth(o, i).start()
 
     for i, (low, count) in enumerate(numbered):
         all_back(i).wait_recv()
@@ -462,14 +491,12 @@
             def _(o=o, i=i):
                 copy_forth(o, i).start()
 
-        for o in upper:
-            copy_forth(o, i).start()
-        for o in lower:
-
-            @pl.when(partner[o] > me_p)
-            def _(o=o, i=i):
-                copy_forth(o, i).start()
-
+        if i == last:
+            pl.when(around)(lambda: near_forth(last - 1))
+        if i == last - 1:
+            pl.when(jnp.logical_not(around))(lambda: near_forth(last - 1))
+        else:
+            near_forth(i)
 
     def spread(left, named, t):
         right = jnp.concatenate(
@@ -488,6 +515,13 @@
                 value = sums[:, i * tile_len : (i + 1) * tile_len]
                 mixed[t + i] = value if fresh else value + mixed[t + i]
 
+    def by_member(value, n):
+        for g in range(level_len):
+            place = pl.ds(pl.multiple_of(level_of(g) * members, members), members)
+            coarse[n, place] = value[g * members : (g + 1) * members]
+        lines = [coarse[n, pl.ds(m, level_len, stride=members), :] for m in range(members)]
+        return jnp.concatenate(lines, axis=0).astype(BF16)
+
     def received(group):
         return jnp.concatenate(
             [side_by_side(arrived.at[o], most, 0, rows) for o in group], axis=1
@@ -503,31 +537,32 @@
     all_forth(0, link_len // 2, 0).wait_recv()
     add(received(upper), entries_of(upper), False)
     for t in range(tiles):
-        base_out[t] = jnp.dot(mixed[t].astype(BF16), interp[t], preferred_element_type=F32)
+        part = by_member(mixed[t], t)
+        base_out[t] = jnp.dot(part, interp[t], preferred_element_type=F32)
     all_forth(link_len // 2, link_len // 2, 1).wait_recv()
-    left_out[...] = received(lower)
+    for n, (o, s) in enumerate((o, s) for o in lower for s in range(most)):
+        value = by_member(arrived[o, s].astype(F32), n)
+        left_out[:, n * tile_len : (n + 1) * tile_len] = value
     for i in range(len(numbered)):
         all_back(i).wait_send()
     all_forth(0, link_len, 0).wait_send()
 
     @pl.when(me_l > 0)
     def _():
-        all_down.wait_send()
+        down.wait_send()
 
     @pl.when(me_l < n_lev - 1)
     def _():
-        all_up.wait_send()
-
-
-def finish(places, left, turn, base, out_hbm, out, sem):
+        up.wait_send()
+
+
+def finish(left, turn, base, out_hbm, out, sem):
     tiles, _, fine = turn.shape
-    level_len = out.shape[1]
     copies = []
     for t in range(tiles):
         sums = base[t] + jnp.dot(left[...], turn[t], preferred_element_type=F32)
         columns = pl.ds(t * fine, fine)
-        for row, level in places:
-            out[:, level, columns] = sums[row : row + out.shape[0]]
+        out[:, :, columns] = sums.reshape(out.shape[0], out.shape[1], fine)
         copy = pltpu.make_async_copy(out.at[:, :, columns], out_hbm.at[:, :, columns], sem.at[t])
         copy.start()
         copies.append(copy)
@@ -549,18 +584,14 @@
         entries = tiles + link_len * most
         words = -(-entries // (31 // k_len.bit_length()))
         weight, send = vert_weight.T, send_tiles.transpose(0, 2, 1)
-        edge = 2 * wide * members
-        sizes = [count for part in chunks_of([(0, rows - edge), (rows - edge, edge)]) for _, count in part]
+        parts = split_rows(n_lev, level_len, members, wide)
+        sizes = [count for part in chunks_of(parts) for _, count in part]
 
         def per_link(count, size=rows):
             return pltpu.VMEM((link_len, count, size, tile_len), BF16)
 
         vmem_spec = pl.BlockSpec(memory_space=pltpu.VMEM)
         half_len = link_len // 2 * most * tile_len
-        order = list(range(wide, level_len - wide))
-        order += list(range(wide)) + list(range(level_len - wide, level_len))
-        places = [(i * members, level) for i, level in enumerate(order)]
-
         left, turn, base = pl.pallas_call(
             functools.partial(kernel, n_patch, n_lev),
             name="localize",
@@ -604,7 +635,7 @@
             compiler_params=pltpu.CompilerParams(collective_id=0, has_side_effects=True),
         )(fields, interp, conv_weight, weight, send, tile_pattern)
         return pl.pallas_call(
-            functools.partial(finish, places),
+            finish,
             name="finish",
             out_shape=jax.ShapeDtypeStruct(fields.shape, F32),
             in_specs=[vmem_spec] * 3,

time: 19.2 us -> 18.2 us (0.948)
  Pallas kernels: 19.1 us -> 18.1 us
    pallas_call x1, Pallas kernels: 17.6 us -> 16.8 us  [shards(): pl.pallas_call(functools.partial(kernel, n_patch, n_lev), name='localize'...]
where the time goes in v6:
time: 18.2 us; the launch traced here: 18.1 us
  Pallas kernels  18.1 us (99%)
    pallas_call x1, Pallas kernels, shards(): pl.pallas_call(functools.partial(kernel, n_patch, n_lev), name='localize'...  16.8 us
    pallas_call x1, Pallas kernels, shards(): pl.pallas_call(finish, name='finish', out_shape=jax.ShapeDtypeStruct(fiel...  1.27 us

profile of v6, /device:TPU:0, one launch (start us, length us, event | category | flops | bytes accessed | tf_op | source)
XLA Modules:
  0.0 18.1 jit_solution(17966264579860156828)
XLA Ops:
  0.0 16.8 %localize.1 = (bf16[128,512]{1,0:T(8,128)(2,1)S(1)}, bf16[8,512,256]{2,1,0:T(8,128)(2,1)S(1)}, f32[8,128,256]{2,1,0:T(8,128)S(1)}) custom-call(bf16[8,16,2048]{2,1,0:T(8,128)(2,1)} %fields_hbm.1, bf16[8,128,256]{2,1,0:T(8,128)(2,1)} %interp_hbm.1, bf16[8,8,128,128]{3,2,1,0:T(8,128)(2,1)} %conv_hbm.1, f32[5,32]{1,0:T(8,128)} %bitcast.2, s32[1,2,4]{2,1,0:T(2,128)} %bitcast.3, ...), custom_call_target="tpu_custom_call" | custom-call | tf_op jit(solution)/shard_map/localize/pallas_call | solution.py:595
  16.8 1.3 %finish.1 = f32[8,16,2048]{2,1,0:T(8,128)} custom-call(bf16[128,512]{1,0:T(8,128)(2,1)S(1)} %get-tuple-element.8.left, bf16[8,512,256]{2,1,0:T(8,128)(2,1)S(1)} %get-tuple-element.9.turn, f32[8,128,256]{2,1,0:T(8,128)S(1)} %get-tuple-element.10.base), custom_call_target="tpu_custom_call" | custom-call | tf_op jit(solution)/shard_map/finish/pallas_call | solution.py:637

commit v7 on v6

--- a/solution.py
+++ b/solution.py
@@ -10,6 +10,7 @@
 MESH = pl.DeviceIdType.MESH
 F32 = jnp.float32
 BF16 = jnp.bfloat16
+VMEM_BYTES = 67043328
 
 
 def link_offsets(reach_len):
@@ -61,10 +62,11 @@
     halo_out,
     halo_in,
     own,
-    mixed,
     smooth,
     ext,
-    power,
+    send_rows,
+    which_made,
+    slot_made,
     which,
     slot_of,
     load_sem,
@@ -117,11 +119,13 @@
 
     load_w = pltpu.make_async_copy(weight_hbm, weight, load_sem.at[3])
     load_s = pltpu.make_async_copy(send_hbm, send, load_sem.at[4])
+    load_v = pltpu.make_async_copy(send_hbm, send_rows, load_sem.at[6])
     load_p = pltpu.make_async_copy(pattern_hbm, pattern, load_sem.at[5])
     load_f = pltpu.make_async_copy(fields_hbm, fields, load_sem.at[0])
     load_i = pltpu.make_async_copy(interp_hbm, interp, load_sem.at[1])
     load_c = pltpu.make_async_copy(conv_hbm, conv.at[:, pl.ds(0, k_len)], load_sem.at[2])
     load_p.start()
+    load_v.start()
     load_s.start()
     load_w.start()
     load_f.start()
@@ -141,21 +145,16 @@
     def _():
         pl.semaphore_signal(barrier, inc=1, device_id={"lev": me_l + 1}, device_id_type=MESH)
 
-    bits = k_len.bit_length()
-    per_word = 31 // bits
     entries = tiles + link_len * most
-    words = -(-entries // per_word)
-    for e in range(entries):
-        for w in range(words):
-            inside = w * per_word <= e < (w + 1) * per_word
-            power[w, e] = jnp.int32(1 << (bits * (e - w * per_word)) if inside else 0)
     for t in range(tiles):
         conv[t, k_len] = jnp.zeros((tile_len, tile_len), BF16)
     for i, (_, count) in enumerate(numbered):
         for o in range(link_len):
             arrived_back[i][o, most] = jnp.zeros((count, tile_len), BF16)
     ext[tiles] = jnp.zeros((rows, tile_len), BF16)
-    eager = jnp.logical_or(me_p < n_patch - 4, me_p >= n_patch - 2)
+    enter_first = jnp.logical_or(me_p < 4, me_p >= n_patch - 2)
+    enter_last = jnp.logical_and(jnp.logical_not(enter_first), me_p >= n_patch - 4)
+    enter_second = jnp.logical_not(jnp.logical_or(enter_first, enter_last))
 
     def enter():
         before = jnp.where(me_l > 0, 1, 0)
@@ -182,27 +181,26 @@
         def _():
             pl.semaphore_signal(enter_lev, inc=1, device_id={"lev": me_l - 1}, device_id_type=MESH)
 
-    pl.when(eager)(enter)
+    pl.when(enter_first)(enter)
+    load_p.wait()
+    load_v.wait()
+    lane = lax.broadcasted_iota(jnp.int32, (tiles, entries), 1)
+    index = jnp.full((tiles, entries), k_len, jnp.int32)
+    for k in range(k_len):
+        index = jnp.where(pattern[:, k : k + 1] == lane, k, index)
+    which_made[...] = index
+    row = lax.broadcasted_iota(jnp.int32, (tiles, link_len), 0)
+    index = jnp.full((tiles, link_len), most, jnp.int32)
+    for s in range(most):
+        index = jnp.where(send_rows[0, s : s + 1, :] == row, s, index)
+    slot_made[...] = index
+    pl.when(enter_second)(enter)
     load_f.wait()
     load_i.wait()
-    load_p.wait()
-    load_s.wait()
-    load_w.wait()
-    empty = sum(k_len << (bits * i) for i in range(per_word))
-    for t in range(tiles):
-        packed = [jnp.int32(empty) for _ in range(words)]
-        for k in range(k_len):
-            named = pattern[t, k]
-            for w in range(words):
-                packed[w] = packed[w] + jnp.int32(k - k_len) * power[w, named]
-        for e in range(entries):
-            w, place = e // per_word, bits * (e % per_word)
-            which[t, e] = (packed[w] >> place) & ((1 << bits) - 1)
-        for o in range(link_len):
-            index = jnp.int32(most)
-            for s in range(most):
-                index = jnp.where(send[0, s, o] == t, s, index)
-            slot_of[t, o] = index
+    make_which = pltpu.make_async_copy(which_made, which, load_sem.at[7])
+    make_slot = pltpu.make_async_copy(slot_made, slot_of, load_sem.at[8])
+    make_which.start()
+    make_slot.start()
     split = tiles // 2
     below = {"lev": lax.rem(me_l + n_lev - 1, n_lev)}
     above = {"lev": lax.rem(me_l + 1, n_lev)}
@@ -235,7 +233,7 @@
                 high = [levels[level_len + 2 * i + n, some] for n in range(2)]
                 halo_out[1, i, some] = jnp.concatenate(high, axis=1).astype(BF16)
         if h == 0:
-            pl.when(jnp.logical_not(eager))(enter)
+            pl.when(enter_last)(enter)
 
         @pl.when(me_l > 0)
         def _(some=some):
@@ -244,6 +242,7 @@
     start = me_l * level_len
 
     sign = jnp.where(me_l == 0, 1, -1) if two else 1
+    load_w.wait()
 
     def coefficient(level, shift):
         return weight[half + sign * shift, jnp.clip(start + turned_level(level), 0, total_levels - 1)]
@@ -289,6 +288,9 @@
         forward_pair(level)
 
     load_c.wait()
+    load_s.wait()
+    make_which.wait()
+    make_slot.wait()
 
     def gathered(left, first):
         right = jnp.concatenate(
@@ -475,7 +477,20 @@
             def _(o=o):
                 copy_forth(o, i).start()
 
+    def places_of(group):
+        return 0 if group is lower else len(lower) * most * tile_len
+
+    def through_interp(group):
+        named = [tiles + o * most + s for o in group for s in range(most)]
+        rows_of = pl.ds(places_of(group), len(named) * tile_len)
+        for t in range(tiles):
+            stack = jnp.concatenate([conv[t, which[t, e]] for e in named], axis=0)
+            product = jnp.dot(stack, interp[t], preferred_element_type=F32)
+            turn_out[t, rows_of] = product.astype(BF16)
+
     for i, (low, count) in enumerate(numbered):
+        if i == last:
+            through_interp(lower)
         all_back(i).wait_recv()
         for t in range(tiles):
             value = own[t, pl.ds(low, count)]
@@ -508,13 +523,6 @@
         )
         return jnp.dot(left, right, preferred_element_type=F32)
 
-    def add(left, named, fresh):
-        for t in range(0, tiles, 2):
-            sums = spread(left, named, t)
-            for i in range(2):
-                value = sums[:, i * tile_len : (i + 1) * tile_len]
-                mixed[t + i] = value if fresh else value + mixed[t + i]
-
     def by_member(value, n):
         for g in range(level_len):
             place = pl.ds(pl.multiple_of(level_of(g) * members, members), members)
@@ -522,6 +530,13 @@
         lines = [coarse[n, pl.ds(m, level_len, stride=members), :] for m in range(members)]
         return jnp.concatenate(lines, axis=0).astype(BF16)
 
+    def by_member(value, n):
+        for g in range(level_len):
+            place = pl.ds(pl.multiple_of(level_of(g) * members, members), members)
+            coarse[n, place] = value[g * members : (g + 1) * members]
+        lines = [coarse[n, pl.ds(m, level_len, stride=members), :] for m in range(members)]
+        return jnp.concatenate(lines, axis=0).astype(BF16)
+
     def received(group):
         return jnp.concatenate(
             [side_by_side(arrived.at[o], most, 0, rows) for o in group], axis=1
@@ -530,19 +545,20 @@
     def entries_of(group):
         return [tiles + o * most + s for o in group for s in range(most)]
 
-    add(side_by_side(ext, tiles, 0, rows), range(tiles), True)
-    for t in range(tiles):
-        stack = jnp.concatenate([conv[t, which[t, e]] for e in entries_of(lower)], axis=0)
-        turn_out[t] = jnp.dot(stack, interp[t], preferred_element_type=F32).astype(BF16)
-    all_forth(0, link_len // 2, 0).wait_recv()
-    add(received(upper), entries_of(upper), False)
-    for t in range(tiles):
-        part = by_member(mixed[t], t)
-        base_out[t] = jnp.dot(part, interp[t], preferred_element_type=F32)
-    all_forth(link_len // 2, link_len // 2, 1).wait_recv()
-    for n, (o, s) in enumerate((o, s) for o in lower for s in range(most)):
-        value = by_member(arrived[o, s].astype(F32), n)
-        left_out[:, n * tile_len : (n + 1) * tile_len] = value
+    left = side_by_side(ext, tiles, 0, rows)
+    for t in range(0, tiles, 2):
+        sums = spread(left, range(tiles), t)
+        for i in range(2):
+            part = by_member(sums[:, i * tile_len : (i + 1) * tile_len], t + i)
+            base_out[t + i] = jnp.dot(part, interp[t + i], preferred_element_type=F32)
+    through_interp(upper)
+    for group in (lower, upper):
+        for n, (o, s) in enumerate((o, s) for o in group for s in range(most)):
+            if n == 0:
+                first = 0 if group is upper else link_len // 2
+                all_forth(first, link_len // 2, 0 if group is upper else 1).wait_recv()
+            place = places_of(group) + n * tile_len
+            left_out[:, place : place + tile_len] = by_member(arrived[o, s].astype(F32), n)
     for i in range(len(numbered)):
         all_back(i).wait_send()
     all_forth(0, link_len, 0).wait_send()
@@ -582,7 +598,6 @@
         rows = members * level_len
         any_spec = pl.BlockSpec(memory_space=pl.ANY)
         entries = tiles + link_len * most
-        words = -(-entries // (31 // k_len.bit_length()))
         weight, send = vert_weight.T, send_tiles.transpose(0, 2, 1)
         parts = split_rows(n_lev, level_len, members, wide)
         sizes = [count for part in chunks_of(parts) for _, count in part]
@@ -591,13 +606,15 @@
             return pltpu.VMEM((link_len, count, size, tile_len), BF16)
 
         vmem_spec = pl.BlockSpec(memory_space=pltpu.VMEM)
-        half_len = link_len // 2 * most * tile_len
+        wide_len = link_len * most * tile_len
+        spare = VMEM_BYTES - 2 * (rows + tiles * fine) * wide_len - 4 * tiles * rows * fine
+        spare -= 1 << 18
         left, turn, base = pl.pallas_call(
             functools.partial(kernel, n_patch, n_lev),
             name="localize",
             out_shape=[
-                pltpu.VMEM((rows, half_len), BF16),
-                pltpu.VMEM((tiles, half_len, fine), BF16),
+                pltpu.VMEM((rows, wide_len), BF16),
+                pltpu.VMEM((tiles, wide_len, fine), BF16),
                 pltpu.VMEM((tiles, rows, fine), F32),
             ],
             in_specs=[any_spec] * 6,
@@ -605,7 +622,7 @@
             scratch_shapes=[
                 pltpu.SMEM(weight.shape, F32),
                 pltpu.SMEM(send.shape, jnp.int32),
-                pltpu.SMEM(tile_pattern.shape, jnp.int32),
+                pltpu.VMEM(tile_pattern.shape, jnp.int32),
                 pltpu.VMEM(fields.shape, BF16),
                 pltpu.VMEM(interp.shape, BF16),
                 pltpu.VMEM((tiles, k_len + 1, tile_len, tile_len), BF16),
@@ -616,13 +633,14 @@
                 pltpu.VMEM((2, wide // 2, tiles, 2 * members, tile_len), BF16),
                 pltpu.VMEM((2, wide // 2, tiles, 2 * members, tile_len), BF16),
                 pltpu.VMEM((tiles, rows, tile_len), F32),
-                pltpu.VMEM((tiles, rows, tile_len), F32),
                 pltpu.VMEM((tiles, rows, tile_len), BF16),
                 pltpu.VMEM((tiles + 1, rows, tile_len), BF16),
-                pltpu.SMEM((words, entries), jnp.int32),
+                pltpu.VMEM(send.shape, jnp.int32),
+                pltpu.VMEM((tiles, entries), jnp.int32),
+                pltpu.VMEM((tiles, link_len), jnp.int32),
                 pltpu.SMEM((tiles, entries), jnp.int32),
                 pltpu.SMEM((tiles, link_len), jnp.int32),
-                pltpu.SemaphoreType.DMA((6,)),
+                pltpu.SemaphoreType.DMA((9,)),
                 pltpu.SemaphoreType.DMA((4,)),
                 pltpu.SemaphoreType.DMA((2,)),
                 pltpu.SemaphoreType.DMA((len(sizes),)),
@@ -632,7 +650,9 @@
             ]
             + [per_link(most)] * 3
             + [per_link(most + 1, size) for size in sizes],
-            compiler_params=pltpu.CompilerParams(collective_id=0, has_side_effects=True),
+            compiler_params=pltpu.CompilerParams(
+                collective_id=0, has_side_effects=True, vmem_limit_bytes=spare
+            ),
         )(fields, interp, conv_weight, weight, send, tile_pattern)
         return pl.pallas_call(
             finish,

time: 18.2 us -> 18.3 us (level)
    pallas_call x1, Pallas kernels: 1.27 us -> 1.49 us  [shards(): pl.pallas_call(finish, name='finish', out_shape=jax.ShapeDtypeStruct(fiel...]
    pallas_call x1, Pallas kernels: 16.8 us -> 16.6 us  [shards(): pl.pallas_call(functools.partial(kernel, n_patch, n_lev), name='localize'...]
where the time goes in v7:
time: 18.3 us; the launch traced here: 18.1 us
  Pallas kernels  18.1 us (99%)
    pallas_call x1, Pallas kernels, shards(): pl.pallas_call(functools.partial(kernel, n_patch, n_lev), name='localize'...  16.6 us
    pallas_call x1, Pallas kernels, shards(): pl.pallas_call(finish, name='finish', out_shape=jax.ShapeDtypeStruct(fiel...  1.49 us

profile of v7, /device:TPU:0, one launch (start us, length us, event | category | flops | bytes accessed | tf_op | source)
XLA Modules:
  0.0 18.1 jit_solution(13237892165442100979)
XLA Ops:
  0.0 16.6 %localize.1 = (bf16[128,1024]{1,0:T(8,128)(2,1)S(1)}, bf16[8,1024,256]{2,1,0:T(8,128)(2,1)S(1)}, f32[8,128,256]{2,1,0:T(8,128)S(1)}) custom-call(bf16[8,16,2048]{2,1,0:T(8,128)(2,1)} %fields_hbm.1, bf16[8,128,256]{2,1,0:T(8,128)(2,1)} %interp_hbm.1, bf16[8,8,128,128]{3,2,1,0:T(8,128)(2,1)} %conv_hbm.1, f32[5,32]{1,0:T(8,128)} %bitcast.2, ...), custom_call_target="tpu_custom_call" | custom-call | tf_op jit(solution)/shard_map/localize/pallas_call | solution.py:612
  16.6 1.5 %finish.1 = f32[8,16,2048]{2,1,0:T(8,128)} custom-call(bf16[128,1024]{1,0:T(8,128)(2,1)S(1)} %get-tuple-element.8.left, bf16[8,1024,256]{2,1,0:T(8,128)(2,1)S(1)} %get-tuple-element.9.turn, f32[8,128,256]{2,1,0:T(8,128)S(1)} %get-tuple-element.10.base), custom_call_target="tpu_custom_call" | custom-call | tf_op jit(solution)/shard_map/finish/pallas_call | solution.py:657

commit v8 on v7

--- a/solution.py
+++ b/solution.py
@@ -146,12 +146,6 @@
         pl.semaphore_signal(barrier, inc=1, device_id={"lev": me_l + 1}, device_id_type=MESH)
 
     entries = tiles + link_len * most
-    for t in range(tiles):
-        conv[t, k_len] = jnp.zeros((tile_len, tile_len), BF16)
-    for i, (_, count) in enumerate(numbered):
-        for o in range(link_len):
-            arrived_back[i][o, most] = jnp.zeros((count, tile_len), BF16)
-    ext[tiles] = jnp.zeros((rows, tile_len), BF16)
     enter_first = jnp.logical_or(me_p < 4, me_p >= n_patch - 2)
     enter_last = jnp.logical_and(jnp.logical_not(enter_first), me_p >= n_patch - 4)
     enter_second = jnp.logical_not(jnp.logical_or(enter_first, enter_last))
@@ -182,6 +176,12 @@
             pl.semaphore_signal(enter_lev, inc=1, device_id={"lev": me_l - 1}, device_id_type=MESH)
 
     pl.when(enter_first)(enter)
+    for t in range(tiles):
+        conv[t, k_len] = jnp.zeros((tile_len, tile_len), BF16)
+    for i, (_, count) in enumerate(numbered):
+        for o in range(link_len):
+            arrived_back[i][o, most] = jnp.zeros((count, tile_len), BF16)
+    ext[tiles] = jnp.zeros((rows, tile_len), BF16)
     load_p.wait()
     load_v.wait()
     lane = lax.broadcasted_iota(jnp.int32, (tiles, entries), 1)
@@ -387,26 +387,14 @@
         def _():
             pl.semaphore_wait(enter_sem.at[1 if wrapped else 0], later)
 
-    def send_back(c):
-        for o in upper:
+    def send_back(c, group):
+        for o in group:
             sum_back(c, o)
         if c == 0:
-            await_entry(upper + lower, False)
+            await_entry(group, False)
         for i in indices(c):
-            for o in upper:
-                copy_back(o, i).start()
-        if c == 0:
-
-            @pl.when(me_l < n_lev - 1)
-            def _():
-                pl.semaphore_wait(enter_lev, 1)
-                up.start()
-
-        for o in lower:
-            sum_back(c, o)
-        for i in indices(c):
-            for o in lower:
-                if c == 0:
+            for o in group:
+                if c == 0 and group is lower:
 
                     @pl.when(source[o] < me_p)
                     def _(o=o, i=i):
@@ -415,7 +403,14 @@
                 else:
                     copy_back(o, i).start()
 
-    send_back(0)
+    send_back(0, lower)
+
+    @pl.when(me_l < n_lev - 1)
+    def _():
+        pl.semaphore_wait(enter_lev, 1)
+        up.start()
+
+    send_back(0, upper)
     for t in range(tiles):
         for k in range(k_len + 1):
             turned[t, k] = conv[t, k].T
@@ -462,11 +457,21 @@
     for level in late[1]:
         forward_pair(level)
 
-    send_back(1)
+    around = me_p >= n_patch - max(offsets)
+
+    @pl.when(around)
+    def _():
+        send_back(1, upper)
+        send_back(1, lower)
+
+    @pl.when(jnp.logical_not(around))
+    def _():
+        send_back(1, lower)
+        send_back(1, upper)
+
     sum_own()
 
     last = len(numbered) - 1
-    around = me_p >= n_patch - max(offsets)
 
     def near_forth(i):
         for o in upper:
@@ -488,9 +493,13 @@
             product = jnp.dot(stack, interp[t], preferred_element_type=F32)
             turn_out[t, rows_of] = product.astype(BF16)
 
+    def both_through_interp():
+        through_interp(lower)
+        through_interp(upper)
+
     for i, (low, count) in enumerate(numbered):
         if i == last:
-            through_interp(lower)
+            pl.when(me_p < 2)(both_through_interp)
         all_back(i).wait_recv()
         for t in range(tiles):
             value = own[t, pl.ds(low, count)]
@@ -551,7 +560,7 @@
         for i in range(2):
             part = by_member(sums[:, i * tile_len : (i + 1) * tile_len], t + i)
             base_out[t + i] = jnp.dot(part, interp[t + i], preferred_element_type=F32)
-    through_interp(upper)
+    pl.when(me_p >= 2)(both_through_interp)
     for group in (lower, upper):
         for n, (o, s) in enumerate((o, s) for o in group for s in range(most)):
             if n == 0:

time: 18.3 us -> 18.8 us (1.027)
  Pallas kernels: 18.1 us -> 18.6 us
    pallas_call x1, Pallas kernels: 16.6 us -> 17.1 us  [shards(): pl.pallas_call(functools.partial(kernel, n_patch, n_lev), name='localize'...]
where the time goes in v8:
time: 18.8 us; the launch traced here: 18.6 us
  Pallas kernels  18.6 us (99%)
    pallas_call x1, Pallas kernels, shards(): pl.pallas_call(functools.partial(kernel, n_patch, n_lev), name='localize'...  17.1 us
    pallas_call x1, Pallas kernels, shards(): pl.pallas_call(finish, name='finish', out_shape=jax.ShapeDtypeStruct(fiel...  1.49 us

profile of v8, /device:TPU:0, one launch (start us, length us, event | category | flops | bytes accessed | tf_op | source)
XLA Modules:
  0.0 18.6 jit_solution(6818593439405470258)
XLA Ops:
  0.0 17.1 %localize.1 = (bf16[128,1024]{1,0:T(8,128)(2,1)S(1)}, bf16[8,1024,256]{2,1,0:T(8,128)(2,1)S(1)}, f32[8,128,256]{2,1,0:T(8,128)S(1)}) custom-call(bf16[8,16,2048]{2,1,0:T(8,128)(2,1)} %fields_hbm.1, bf16[8,128,256]{2,1,0:T(8,128)(2,1)} %interp_hbm.1, bf16[8,8,128,128]{3,2,1,0:T(8,128)(2,1)} %conv_hbm.1, f32[5,32]{1,0:T(8,128)} %bitcast.2, ...), custom_call_target="tpu_custom_call" | custom-call | tf_op jit(solution)/shard_map/localize/pallas_call | solution.py:621
  17.1 1.5 %finish.1 = f32[8,16,2048]{2,1,0:T(8,128)} custom-call(bf16[128,1024]{1,0:T(8,128)(2,1)S(1)} %get-tuple-element.8.left, bf16[8,1024,256]{2,1,0:T(8,128)(2,1)S(1)} %get-tuple-element.9.turn, f32[8,128,256]{2,1,0:T(8,128)S(1)} %get-tuple-element.10.base), custom_call_target="tpu_custom_call" | custom-call | tf_op jit(solution)/shard_map/finish/pallas_call | solution.py:666

commit v9 on v8

--- a/solution.py
+++ b/solution.py
@@ -515,12 +515,12 @@
             def _(o=o, i=i):
                 copy_forth(o, i).start()
 
-        if i == last:
-            pl.when(around)(lambda: near_forth(last - 1))
-        if i == last - 1:
-            pl.when(jnp.logical_not(around))(lambda: near_forth(last - 1))
+        if i < last:
+            pl.when(jnp.logical_not(around))(functools.partial(near_forth, i))
         else:
-            near_forth(i)
+            for earlier in range(last):
+                pl.when(around)(functools.partial(near_forth, earlier))
+            near_forth(last)
 
     def spread(left, named, t):
         right = jnp.concatenate(

time: 18.8 us -> 18.8 us (level)
  no operation moved by 1% of the time
where the time goes in v9:
time: 18.8 us; the launch traced here: 18.6 us
  Pallas kernels  18.6 us (99%)
    pallas_call x1, Pallas kernels, shards(): pl.pallas_call(functools.partial(kernel, n_patch, n_lev), name='localize'...  17.1 us
    pallas_call x1, Pallas kernels, shards(): pl.pallas_call(finish, name='finish', out_shape=jax.ShapeDtypeStruct(fiel...  1.49 us

profile of v9, /device:TPU:0, one launch (start us, length us, event | category | flops | bytes accessed | tf_op | source)
XLA Modules:
  0.0 18.6 jit_solution(3069836861987410358)
XLA Ops:
  0.0 17.1 %localize.1 = (bf16[128,1024]{1,0:T(8,128)(2,1)S(1)}, bf16[8,1024,256]{2,1,0:T(8,128)(2,1)S(1)}, f32[8,128,256]{2,1,0:T(8,128)S(1)}) custom-call(bf16[8,16,2048]{2,1,0:T(8,128)(2,1)} %fields_hbm.1, bf16[8,128,256]{2,1,0:T(8,128)(2,1)} %interp_hbm.1, bf16[8,8,128,128]{3,2,1,0:T(8,128)(2,1)} %conv_hbm.1, f32[5,32]{1,0:T(8,128)} %bitcast.2, ...), custom_call_target="tpu_custom_call" | custom-call | tf_op jit(solution)/shard_map/localize/pallas_call | solution.py:621
  17.1 1.5 %finish.1 = f32[8,16,2048]{2,1,0:T(8,128)} custom-call(bf16[128,1024]{1,0:T(8,128)(2,1)S(1)} %get-tuple-element.8.left, bf16[8,1024,256]{2,1,0:T(8,128)(2,1)S(1)} %get-tuple-element.9.turn, f32[8,128,256]{2,1,0:T(8,128)S(1)} %get-tuple-element.10.base), custom_call_target="tpu_custom_call" | custom-call | tf_op jit(solution)/shard_map/finish/pallas_call | solution.py:666

commit v10 on v9

--- a/solution.py
+++ b/solution.py
@@ -403,14 +403,14 @@
                 else:
                     copy_back(o, i).start()
 
-    send_back(0, lower)
+    send_back(0, upper)
 
     @pl.when(me_l < n_lev - 1)
     def _():
         pl.semaphore_wait(enter_lev, 1)
         up.start()
 
-    send_back(0, upper)
+    send_back(0, lower)
     for t in range(tiles):
         for k in range(k_len + 1):
             turned[t, k] = conv[t, k].T
@@ -457,30 +457,19 @@
     for level in late[1]:
         forward_pair(level)
 
-    around = me_p >= n_patch - max(offsets)
-
-    @pl.when(around)
+    @pl.when(me_p < 2)
+    def _():
+        send_back(1, lower)
+        send_back(1, upper)
+
+    @pl.when(me_p >= 2)
     def _():
         send_back(1, upper)
         send_back(1, lower)
 
-    @pl.when(jnp.logical_not(around))
-    def _():
-        send_back(1, lower)
-        send_back(1, upper)
-
     sum_own()
 
     last = len(numbered) - 1
-
-    def near_forth(i):
-        for o in upper:
-            copy_forth(o, i).start()
-        for o in lower:
-
-            @pl.when(partner[o] > me_p)
-            def _(o=o):
-                copy_forth(o, i).start()
 
     def places_of(group):
         return 0 if group is lower else len(lower) * most * tile_len
@@ -515,12 +504,13 @@
             def _(o=o, i=i):
                 copy_forth(o, i).start()
 
-        if i < last:
-            pl.when(jnp.logical_not(around))(functools.partial(near_forth, i))
-        else:
-            for earlier in range(last):
-                pl.when(around)(functools.partial(near_forth, earlier))
-            near_forth(last)
+        for o in upper:
+            copy_forth(o, i).start()
+        for o in lower:
+
+            @pl.when(partner[o] > me_p)
+            def _(o=o, i=i):
+                copy_forth(o, i).start()
 
     def spread(left, named, t):
         right = jnp.concatenate(

time: 18.8 us -> 18.2 us (0.968)
  Pallas kernels: 18.6 us -> 18 us
    pallas_call x1, Pallas kernels: 17.1 us -> 16.5 us  [shards(): pl.pallas_call(functools.partial(kernel, n_patch, n_lev), name='localize'...]
where the time goes in v10:
time: 18.2 us; the launch traced here: 18 us
  Pallas kernels  18 us (99%)
    pallas_call x1, Pallas kernels, shards(): pl.pallas_call(functools.partial(kernel, n_patch, n_lev), name='localize'...  16.5 us
    pallas_call x1, Pallas kernels, shards(): pl.pallas_call(finish, name='finish', out_shape=jax.ShapeDtypeStruct(fiel...  1.49 us

profile of v10, /device:TPU:0, one launch (start us, length us, event | category | flops | bytes accessed | tf_op | source)
XLA Modules:
  0.0 18.0 jit_solution(15254210355041940899)
XLA Ops:
  0.0 16.5 %localize.1 = (bf16[128,1024]{1,0:T(8,128)(2,1)S(1)}, bf16[8,1024,256]{2,1,0:T(8,128)(2,1)S(1)}, f32[8,128,256]{2,1,0:T(8,128)S(1)}) custom-call(bf16[8,16,2048]{2,1,0:T(8,128)(2,1)} %fields_hbm.1, bf16[8,128,256]{2,1,0:T(8,128)(2,1)} %interp_hbm.1, bf16[8,8,128,128]{3,2,1,0:T(8,128)(2,1)} %conv_hbm.1, f32[5,32]{1,0:T(8,128)} %bitcast.2, ...), custom_call_target="tpu_custom_call" | custom-call | tf_op jit(solution)/shard_map/localize/pallas_call | solution.py:611
  16.5 1.5 %finish.1 = f32[8,16,2048]{2,1,0:T(8,128)} custom-call(bf16[128,1024]{1,0:T(8,128)(2,1)S(1)} %get-tuple-element.8.left, bf16[8,1024,256]{2,1,0:T(8,128)(2,1)S(1)} %get-tuple-element.9.turn, f32[8,128,256]{2,1,0:T(8,128)S(1)} %get-tuple-element.10.base), custom_call_target="tpu_custom_call" | custom-call | tf_op jit(solution)/shard_map/finish/pallas_call | solution.py:656

commit v11 on v10

--- a/solution.py
+++ b/solution.py
@@ -197,8 +197,8 @@
     pl.when(enter_second)(enter)
     load_f.wait()
     load_i.wait()
-    make_which = pltpu.make_async_copy(which_made, which, load_sem.at[7])
-    make_slot = pltpu.make_async_copy(slot_made, slot_of, load_sem.at[8])
+    make_which = pltpu.make_async_copy(which_made, which, load_sem.at[5])
+    make_slot = pltpu.make_async_copy(slot_made, slot_of, load_sem.at[6])
     make_which.start()
     make_slot.start()
     split = tiles // 2
@@ -551,7 +551,7 @@
             part = by_member(sums[:, i * tile_len : (i + 1) * tile_len], t + i)
             base_out[t + i] = jnp.dot(part, interp[t + i], preferred_element_type=F32)
     pl.when(me_p >= 2)(both_through_interp)
-    for group in (lower, upper):
+    for group in (upper, lower):
         for n, (o, s) in enumerate((o, s) for o in group for s in range(most)):
             if n == 0:
                 first = 0 if group is upper else link_len // 2
@@ -639,8 +639,8 @@
                 pltpu.VMEM((tiles, link_len), jnp.int32),
                 pltpu.SMEM((tiles, entries), jnp.int32),
                 pltpu.SMEM((tiles, link_len), jnp.int32),
-                pltpu.SemaphoreType.DMA((9,)),
-                pltpu.SemaphoreType.DMA((4,)),
+                pltpu.SemaphoreType.DMA((7,)),
+                pltpu.SemaphoreType.DMA((2 if n_lev == 2 else 4,)),
                 pltpu.SemaphoreType.DMA((2,)),
                 pltpu.SemaphoreType.DMA((len(sizes),)),
                 pltpu.SemaphoreType.DMA((2,)),

time: 18.2 us -> 18.1 us (level)
  no operation moved by 1% of the time
where the time goes in v11:
time: 18.1 us; the launch traced here: 17.9 us
  Pallas kernels  17.9 us (99%)
    pallas_call x1, Pallas kernels, shards(): pl.pallas_call(functools.partial(kernel, n_patch, n_lev), name='localize'...  16.4 us
    pallas_call x1, Pallas kernels, shards(): pl.pallas_call(finish, name='finish', out_shape=jax.ShapeDtypeStruct(fiel...  1.49 us

profile of v11, /device:TPU:0, one launch (start us, length us, event | category | flops | bytes accessed | tf_op | source)
XLA Modules:
  0.0 17.9 jit_solution(404496433030639760)
XLA Ops:
  0.0 16.4 %localize.1 = (bf16[128,1024]{1,0:T(8,128)(2,1)S(1)}, bf16[8,1024,256]{2,1,0:T(8,128)(2,1)S(1)}, f32[8,128,256]{2,1,0:T(8,128)S(1)}) custom-call(bf16[8,16,2048]{2,1,0:T(8,128)(2,1)} %fields_hbm.1, bf16[8,128,256]{2,1,0:T(8,128)(2,1)} %interp_hbm.1, bf16[8,8,128,128]{3,2,1,0:T(8,128)(2,1)} %conv_hbm.1, f32[5,32]{1,0:T(8,128)} %bitcast.2, ...), custom_call_target="tpu_custom_call" | custom-call | tf_op jit(solution)/shard_map/localize/pallas_call | solution.py:611
  16.4 1.5 %finish.1 = f32[8,16,2048]{2,1,0:T(8,128)} custom-call(bf16[128,1024]{1,0:T(8,128)(2,1)S(1)} %get-tuple-element.8.left, bf16[8,1024,256]{2,1,0:T(8,128)(2,1)S(1)} %get-tuple-element.9.turn, f32[8,128,256]{2,1,0:T(8,128)S(1)} %get-tuple-element.10.base), custom_call_target="tpu_custom_call" | custom-call | tf_op jit(solution)/shard_map/finish/pallas_call | solution.py:656

commit v12 on v11

--- a/solution.py
+++ b/solution.py
@@ -23,7 +23,7 @@
 def chunks_of(parts):
     chunks = []
     for low, count in parts:
-        step = 32 if count % 32 == 0 else count
+        step = next((n for n in (32, 16) if count % n == 0 and count > n), count)
         chunks.append([(low + at, step) for at in range(0, count, step)])
     return chunks
 

time: 18.1 us -> 18.1 us (level)
  no operation moved by 1% of the time
where the time goes in v12:
time: 18.1 us; the launch traced here: 17.9 us
  Pallas kernels  17.9 us (99%)
    pallas_call x1, Pallas kernels, shards(): pl.pallas_call(functools.partial(kernel, n_patch, n_lev), name='localize'...  16.4 us
    pallas_call x1, Pallas kernels, shards(): pl.pallas_call(finish, name='finish', out_shape=jax.ShapeDtypeStruct(fiel...  1.49 us

profile of v12, /device:TPU:0, one launch (start us, length us, event | category | flops | bytes accessed | tf_op | source)
XLA Modules:
  0.0 17.9 jit_solution(2514145963730644846)
XLA Ops:
  0.0 16.4 %localize.1 = (bf16[128,1024]{1,0:T(8,128)(2,1)S(1)}, bf16[8,1024,256]{2,1,0:T(8,128)(2,1)S(1)}, f32[8,128,256]{2,1,0:T(8,128)S(1)}) custom-call(bf16[8,16,2048]{2,1,0:T(8,128)(2,1)} %fields_hbm.1, bf16[8,128,256]{2,1,0:T(8,128)(2,1)} %interp_hbm.1, bf16[8,8,128,128]{3,2,1,0:T(8,128)(2,1)} %conv_hbm.1, f32[5,32]{1,0:T(8,128)} %bitcast.2, ...), custom_call_target="tpu_custom_call" | custom-call | tf_op jit(solution)/shard_map/localize/pallas_call | solution.py:611
  16.5 1.5 %finish.1 = f32[8,16,2048]{2,1,0:T(8,128)} custom-call(bf16[128,1024]{1,0:T(8,128)(2,1)S(1)} %get-tuple-element.8.left, bf16[8,1024,256]{2,1,0:T(8,128)(2,1)S(1)} %get-tuple-element.9.turn, f32[8,128,256]{2,1,0:T(8,128)S(1)} %get-tuple-element.10.base), custom_call_target="tpu_custom_call" | custom-call | tf_op jit(solution)/shard_map/finish/pallas_call | solution.py:656
